TPU v7x, 32 devices: a whole 2x2x4 slice. The times are simulated.
32 devices in a mesh: row: 8 (over y, x, core), col: 4 (over z).
Axes of the slice: x: 2, y: 2, z: 4, core: 2. Of those that a mesh axis runs over, the one named last changes fastest.
Arguments:
- state: float32 [2048, 4, 1024], P('row', 'col'), may hold values from -6 to 6
- coupling: bfloat16 [2048, 4, 1024], P('row', 'col'), may hold values from -2 to 2, as said below
- coupling_t: bfloat16 [2, 2048, 4, 1024], P(None, 'row', 'col'), may hold values from -2 to 2, as said below
- factor: float32 [4, 4, 256, 256], P(None, 'col', 'row'), may hold values from -0.3 to 1.3
- cofactor: float32 [4, 4, 256, 256], P(None, 'col', 'row'), may hold values from -0.3 to 1.3
- rates: float32 [4, 4, 256], P(None, 'col'), may hold values from 0.5 to 2
Outputs:
- updated_state: float32 [2048, 4, 1024], P('row', 'col')
Inputs may be any that keep to these rules, and one draw needn't show every extreme that they name: coupling and coupling_t hold the same matrix A; its blocks A(i, k) are zero unless k > i. coupling_t holds the transposed blocks of the A in coupling.
All inputs are finite; a program needn't handle non-finite values.
Results may differ from a plain program's by a relative error of at most 0.0003.
Values may be sent and summed in bfloat16 or wider, within the bound.
A program may use at most 64 MiB of HBM per device.

v0:
```python
import functools

import jax
import jax.numpy as jnp
from jax import lax
from jax.experimental import pallas as pl
from jax.experimental.pallas import tpu as pltpu
from jax.sharding import PartitionSpec as P

STEPS = 2
CHUNKS = 4
MESH = pl.DeviceIdType.MESH
F32 = jnp.float32
NN = (((1,), (0,)), ((), ()))
NT = (((1,), (1,)), ((), ()))


def halves(x):
    hi = x.astype(jnp.bfloat16)
    return hi, (x - hi.astype(F32)).astype(jnp.bfloat16)


def mm(a, b, dims):
    return lax.dot_general(a, b, dims, preferred_element_type=F32)


def dot3(a, b, dims):
    ah, al = halves(a)
    bh, bl = halves(b)
    return mm(ah, bh, dims) + (mm(ah, bl, dims) + mm(al, bh, dims))


def kernel(R, C, U, BS, SR, state, upper, lower, factor, cofactor, rates, out,
           ops, ebuf, xz, atb, an, ops_sem, e_sem, xz_sem, at_sem, an_sem, send_sem):
    H = R // 2
    r = lax.axis_index("row")
    c = lax.axis_index("col")
    d = [2 * R - 1 - s for s in range(STEPS)]

    def owner(row, s):
        return (d[s] - row) % C

    o = [owner(r, s) for s in range(STEPS)]
    sends = []
    me = r * C + c

    barrier = pltpu.get_barrier_semaphore()

    @pl.loop(1, R * C)
    def _(k):
        peer = (me + k) % (R * C)
        pl.semaphore_signal(barrier, inc=1, device_id=(peer // C, peer % C), device_id_type=MESH)

    pl.semaphore_wait(barrier, R * C - 1)

    def send(cond, src, dst, sem, dev):
        k = len(sends)
        copy = pltpu.make_async_remote_copy(
            src_ref=src, dst_ref=dst, send_sem=send_sem.at[k], recv_sem=sem,
            device_id=dev, device_id_type=MESH)
        sends.append((cond, copy))

        @pl.when(cond)
        def _():
            copy.start()

    def send_or_local(cond, src, dst, sem, dev):
        mine = (dev[0] == r) & (dev[1] == c)
        send(cond & jnp.logical_not(mine), src, dst, sem, dev)

        @pl.when(cond & mine)
        def _():
            pltpu.make_async_copy(src, dst, sem).start()

    def arrive(ref, sem):
        pltpu.make_async_copy(ref, ref, sem).wait()

    def slot(u):
        if isinstance(u, int):
            return pl.ds(u * BS, BS)
        return pl.ds(pl.multiple_of(u * BS, BS), BS)

    def target(row, m, s):
        return (row <= m) & (row + m < d[s])

    rows = pl.ds(pl.multiple_of(r * SR, SR), SR)

    def send_operators(s):
        for src, base in ((cofactor, 0), (factor, 2)):
            for u in range(U):
                m = c + C * u
                if u >= U // 2 - s:
                    to = d[s] - m
                    send_or_local((to >= 0) & (to < R), src.at[u], ops.at[base + 1, rows],
                                  ops_sem.at[base + 1], (to, c))
                if u < U // 2:
                    send_or_local(m < R, src.at[u], ops.at[base, rows],
                                  ops_sem.at[base], (m, owner(m, s)))

    def from_upper(u):
        return (u + 1) * C <= H

    def send_lower(s, slots):
        to = (r + R - s - H) % R
        for u in slots:
            if not from_upper(u):
                m = c + C * u
                send(target(to, m, s) & (to + s < R), lower.at[0, :, slot(u)], atb.at[s, u],
                     at_sem.at[s, u], (to, c))

    def send_plain(s):
        m = r
        to_u = jnp.minimum(m // C, U - 1)
        for u in range(H // C + 1):
            i = c + C * u - s
            reach = (i >= 0) & (m < (H // C) * C) & target(i, m, s)
            send_or_local(reach, upper.at[:, slot(u)], atb.at[s, to_u],
                          at_sem.at[s, to_u], (i, m % C))

    def send_upper():
        for u in range(U):
            m = c + C * u - 1
            to = (c + C - 1) % C
            to_u = jnp.maximum(jnp.where(c >= 1, u, u - 1), 0)
            send((m >= 0) & target(r, m, 1), upper.at[:, slot(u)], an.at[to_u],
                 an_sem.at[to_u], (r, to))

    for s in range(STEPS):
        send_or_local(c == r % C, rates, ebuf, e_sem.at[0], (r, o[s]))
    send_operators(0)
    send_operators(1)
    send_upper()
    send_lower(0, range(U - 1, U // 2 - 1, -1))
    send_plain(0)
    out[...] = state[...]

    def spread(s, h, who):
        own_col = r % C == c
        k = jnp.where(own_col, r // C, (d[s] - r) // C)
        has = (own_col | (c == o[s])) & who

        def give(cond, to):
            send(cond & has, xz.at[s, U, part(h)], xz.at[s, k, part(h)], xz_sem.at[s, k, h], (to, c))

        give(r % 2 == 1, jnp.maximum(r - 1, 0))
        for back in range(1, R // 2):
            pair = r // 2 - back
            give(pair >= 0, jnp.maximum(2 * pair + 1 - r % 2, 0))

    def part(h):
        return pl.ds(h * (BS // CHUNKS), BS // CHUNKS)

    def pass_row(s, h, who=True):
        block = xz.at[s, U, part(h)]
        sem = xz_sem.at[s, U, h]
        far = o[s] == 0
        up = (c >= o[s]) & (c < C - 1)
        if s == 0:
            send((c == o[s]) & far & who, block, block, sem, (r, C - 1))
            up = up & jnp.logical_not(far & (c == C - 2))
        send((c <= o[s]) & (c >= 1) & who, block, block, sem, (r, jnp.maximum(c - 1, 0)))
        send(up & who, block, block, sem, (r, jnp.minimum(c + 1, C - 1)))

    def take_row(s):
        other = c != o[s]
        for h in range(CHUNKS):
            @pl.when(other)
            def _(h=h):
                arrive(xz.at[s, U, part(h)], xz_sem.at[s, U, h])

            pass_row(s, h, other)
            spread(s, h, other)

    def give_row(s):
        for h in range(CHUNKS):
            pass_row(s, h, c == o[s])
            spread(s, h, c == o[s])

    def solve(s):
        q = (d[s] - r) // C
        arrive(ebuf, e_sem.at[0])
        left_e = jnp.transpose(jnp.broadcast_to(ebuf[pl.ds(r // C, 1), :], (BS, BS)))
        rate = left_e + rates[pl.ds(q, 1), :]
        arrive(ops.at[0], ops_sem.at[0])
        mid = dot3(ops[0], out[:, slot(q)], NN)
        arrive(ops.at[1], ops_sem.at[1])
        mid = dot3(mid, ops[1], NT) / rate
        arrive(ops.at[2], ops_sem.at[2])
        mid = dot3(ops[2], mid, NN)
        arrive(ops.at[3], ops_sem.at[3])
        x = -dot3(mid, ops[3], NT)
        xz[s, U] = x
        out[:, slot(q)] = x

    def z_index(u, s):
        m = c + C * u
        j = jnp.where(d[s] - m <= m, d[s] - m, m)
        k = jnp.where(j == r, U, jnp.where(j % C == c, j // C, u))
        return j, k

    def collect(u, s, extra=True):
        j, k = z_index(u, s)
        landed = r < j
        if u >= U // 2:
            landed = landed & (j % C != c)
        landed = landed & extra

        for h in range(CHUNKS):
            block = xz.at[s, u, part(h)]

            @pl.when(landed)
            def _(block=block, h=h):
                arrive(block, xz_sem.at[s, u, h])

            send(landed & (r // 2 < j // 2) & (r % 2 != j % 2), block, block,
                 xz_sem.at[s, u, h], (r + 1 - 2 * (r % 2), c))

    def right(u, s):
        arrive(atb.at[s, u], at_sem.at[s, u])
        xh, xl = halves(xz[s, U])
        at = atb[s, u]
        dims = NT if from_upper(u) else NN
        out[:, slot(u)] -= mm(xh, at, dims) + mm(xl, at, dims)

    def left(u, s):
        m = c + C * u
        j, k = z_index(u, s)
        if s > 0:
            arrive(an.at[u], an_sem.at[u])
            a = an[u]
        else:
            a = upper[:, slot(u)]
        zh, zl = halves(xz[s, k])

        def apply(dims):
            out[:, slot(u)] -= mm(a, zh, dims) + mm(a, zl, dims)

        low, high = C * u, C * u + C - 1
        if 2 * low >= d[s]:
            apply(NN)
        elif 2 * high < d[s]:
            apply(NT)
        else:
            straight = d[s] - m <= m
            pl.when(straight)(lambda: apply(NN))
            pl.when(jnp.logical_not(straight))(lambda: apply(NT))

    def on_targets(s, fns, but=None):
        for u in range(U):
            live = target(r, c + C * u, s)
            if but is not None:
                live = live & jnp.logical_not(but(u))

            @pl.when(live)
            def _(u=u):
                for fn in fns:
                    fn(u, s)

    @pl.when(c == o[0])
    def _():
        solve(0)

    give_row(0)
    take_row(0)
    send_lower(0, range(U // 2 - 1, -1, -1))
    send_lower(1, range(U - 1, -1, -1))
    send_plain(1)

    q1 = (d[1] - r) // C
    first = c == o[1]

    def picked(u):
        return first & (q1 == u)

    for u in range(U // 2 - 1, U):
        collect(u, 0, picked(u))

        @pl.when(picked(u))
        def _(u=u):
            right(u, 0)
            left(u, 0)

    @pl.when(first)
    def _():
        solve(1)

    give_row(1)

    def rest():
        on_targets(0, (right, left), picked)

    for u in range(U):
        collect(u, 0, jnp.logical_not(picked(u)))
    rest()

    take_row(1)
    on_targets(1, (right,))
    for u in range(U):
        collect(u, 1)
    on_targets(1, (left,))

    for cond, copy in sends:
        @pl.when(cond)
        def _(copy=copy):
            copy.wait_send()


def on_device(state, coupling, coupling_t, factor, cofactor, rates):
    R = lax.axis_size("row")
    C = lax.axis_size("col")
    U = 2 * R // C
    BS = state.shape[0]
    SR = factor.shape[2]
    flat = U * BS
    vmem = pl.BlockSpec(memory_space=pltpu.VMEM)
    hbm = pl.BlockSpec(memory_space=pl.ANY)
    n_sends = 2 * STEPS * (2 * U) + (STEPS + 8) * (2 * U) + STEPS * CHUNKS * (R + 2 * U + 8)
    dma = pltpu.SemaphoreType.DMA
    out = pl.pallas_call(
        functools.partial(kernel, R, C, U, BS, SR),
        out_shape=jax.ShapeDtypeStruct((BS, flat), F32),
        in_specs=[vmem, vmem, hbm, vmem, vmem, vmem],
        out_specs=vmem,
        scratch_shapes=[
            pltpu.VMEM((4, BS, BS), F32),
            pltpu.VMEM((U, BS), F32),
            pltpu.VMEM((STEPS, U + 1, BS, BS), F32),
            pltpu.VMEM((STEPS, U, BS, BS), jnp.bfloat16),
            pltpu.VMEM((U, BS, BS), jnp.bfloat16),
            dma((4,)),
            dma((1,)),
            dma((STEPS, U + 1, CHUNKS)),
            dma((STEPS, U)),
            dma((U,)),
            dma((n_sends,)),
        ],
        compiler_params=pltpu.CompilerParams(
            collective_id=0, has_side_effects=True, vmem_limit_bytes=48 * 1024 * 1024),
    )(
        state.reshape(BS, flat),
        coupling.reshape(BS, flat),
        coupling_t.reshape(coupling_t.shape[0], BS, flat),
        factor.reshape(U, SR, BS),
        cofactor.reshape(U, SR, BS),
        rates.reshape(U, BS),
    )
    return out.reshape(BS, 1, flat)


def solution(mesh):
    return jax.shard_map(
        on_device,
        mesh=mesh,
        in_specs=(
            P("row", "col", None),
            P("row", "col", None),
            P(None, "row", "col", None),
            P(None, "col", "row", None),
            P(None, "col", "row", None),
            P(None, "col", None),
        ),
        out_specs=P("row", "col", None),
        check_vma=False,
    )
```

profile of v0, /device:TPU:16, one launch (start us, length us, event | category | flops | bytes accessed | tf_op | source)
XLA Modules:
  0.0 60.2 jit_solution(8813636587969967112)
XLA Ops:
  0.0 0.0 copy-start.4
  0.0 0.7 %copy-done.4 = f32[4,1,256]{2,1,0:T(1,128)S(1)} copy-done((f32[4,1,256]{2,1,0:T(1,128)S(1)}, f32[4,1,256]{2,1,0:T(1,128)}, u32[]{:S(2)}) %copy-start.4) | copy-done | bytes 4120
  0.7 0.0 copy-start
  0.7 0.0 copy-start.1
  0.7 0.0 copy-start.2
  0.7 0.0 copy-start.3
  0.7 1.6 %copy.12 = f32[256,1,1024]{2,0,1:T(8,128)S(1)} copy(f32[256,1,1024]{2,1,0:T(1,128)} %param.6) | data formatting | bytes 2097152
  2.3 0.0 copy-done
  2.3 0.1 copy-done.1
  2.4 0.0 copy-done.2
  2.4 0.0 copy-done.3
  2.4 55.7 %shard_map.64 = f32[256,1024]{1,0:T(8,128)S(1)} custom-call(f32[256,1024]{1,0:T(8,128)S(1)} %bitcast.12, bf16[256,1024]{1,0:T(8,128)(2,1)S(1)} %bitcast.14, bf16[2,256,1024]{2,1,0:T(8,128)(2,1)S(1)} %bitcast.13, f32[4,32,256]{2,1,0:T(8,128)S(1)} %bitcast.15, f32[4,32,256]{2,1,0:T(8,128)S(1)} %bitcast.16, f32[4,256]{1,0:T(4,128)S(1)} %bitcast.17), custom_call_target="tpu_custom_call" | custom-call | tf_op jit(solution)/shard_map/pallas_call | solution.py:319
  58.1 2.0 %copy.7 = f32[256,1,1024]{2,1,0:T(1,128)} copy(f32[256,1,1024]{2,0,1:T(8,128)S(1)} %bitcast.11) | data formatting | bytes 2097152 | tf_op jit(solution)/shard_map/reshape | solution.py:347
  (1 shorter events, 0.0 us)
Async XLA Ops:
  0.0 0.7 %copy-start.4 = (f32[4,1,256]{2,1,0:T(1,128)S(1)}, f32[4,1,256]{2,1,0:T(1,128)}, u32[]{:S(2)}) copy-start(f32[4,1,256]{2,1,0:T(1,128)} %param.11) | copy-start | bytes 12292
  0.7 1.6 %copy-start = (bf16[2,256,1,1024]{3,1,2,0:T(8,128)(2,1)S(1)}, bf16[2,256,1,1024]{3,1,2,0:T(8,128)(2,1)}, u32[]{:S(2)}) copy-start(bf16[2,256,1,1024]{3,1,2,0:T(8,128)(2,1)} %param.8) | copy-start | bytes 3145732
  0.7 1.7 %copy-start.1 = (bf16[256,1,1024]{2,0,1:T(8,128)(2,1)S(1)}, bf16[256,1,1024]{2,0,1:T(8,128)(2,1)}, u32[]{:S(2)}) copy-start(bf16[256,1,1024]{2,0,1:T(8,128)(2,1)} %param.7) | copy-start | bytes 1572868
  0.7 1.7 %copy-start.2 = (f32[4,1,32,256]{3,2,1,0:T(8,128)S(1)}, f32[4,1,32,256]{3,2,1,0:T(8,128)}, u32[]{:S(2)}) copy-start(f32[4,1,32,256]{3,2,1,0:T(8,128)} %param.9) | copy-start | bytes 393220
  0.7 1.7 %copy-start.3 = (f32[4,1,32,256]{3,2,1,0:T(8,128)S(1)}, f32[4,1,32,256]{3,2,1,0:T(8,128)}, u32[]{:S(2)}) copy-start(f32[4,1,32,256]{3,2,1,0:T(8,128)} %param.10) | copy-start | bytes 393220
where the time goes:
time: 60.3 us; the launch traced here: 60.2 us
  Pallas kernels  55.7 us (92%)
  local copies, waits for them, and re-layouts  4.44 us (7%)
    pallas_call x1, Pallas kernels, on_device(): pl.pallas_call(functools.partial(kernel, R, C, U, BS, SR), out_shape=jax....  55.7 us
    unnamed x12, local copies, waits for them, and re-layouts  2.4 us
    reshape x1, local copies, waits for them, and re-layouts, on_device(): return out.reshape(BS, 1, flat)  2.05 us

commit v1 on v0

--- a/solution.py
+++ b/solution.py
@@ -54,9 +54,8 @@
     pl.semaphore_wait(barrier, R * C - 1)
 
     def send(cond, src, dst, sem, dev):
-        k = len(sends)
         copy = pltpu.make_async_remote_copy(
-            src_ref=src, dst_ref=dst, send_sem=send_sem.at[k], recv_sem=sem,
+            src_ref=src, dst_ref=dst, send_sem=send_sem.at[0], recv_sem=sem,
             device_id=dev, device_id_type=MESH)
         sends.append((cond, copy))
 
@@ -128,9 +127,8 @@
     for s in range(STEPS):
         send_or_local(c == r % C, rates, ebuf, e_sem.at[0], (r, o[s]))
     send_operators(0)
+    send_lower(0, range(U - 1, U // 2 - 1, -1))
     send_operators(1)
-    send_upper()
-    send_lower(0, range(U - 1, U // 2 - 1, -1))
     send_plain(0)
     out[...] = state[...]
 
@@ -262,6 +260,7 @@
 
     give_row(0)
     take_row(0)
+    send_upper()
     send_lower(0, range(U // 2 - 1, -1, -1))
     send_lower(1, range(U - 1, -1, -1))
     send_plain(1)
@@ -314,7 +313,6 @@
     flat = U * BS
     vmem = pl.BlockSpec(memory_space=pltpu.VMEM)
     hbm = pl.BlockSpec(memory_space=pl.ANY)
-    n_sends = 2 * STEPS * (2 * U) + (STEPS + 8) * (2 * U) + STEPS * CHUNKS * (R + 2 * U + 8)
     dma = pltpu.SemaphoreType.DMA
     out = pl.pallas_call(
         functools.partial(kernel, R, C, U, BS, SR),
@@ -332,7 +330,7 @@
             dma((STEPS, U + 1, CHUNKS)),
             dma((STEPS, U)),
             dma((U,)),
-            dma((n_sends,)),
+            dma((1,)),
         ],
         compiler_params=pltpu.CompilerParams(
             collective_id=0, has_side_effects=True, vmem_limit_bytes=48 * 1024 * 1024),

time: 60.3 us -> 57.8 us (0.959)
  the two profiles are of different devices: /device:TPU:16 before, /device:TPU:2 now
where the time goes in v1:
time: 57.8 us; the launch traced here: 57.7 us
  Pallas kernels  53.2 us (92%)
  local copies, waits for them, and re-layouts  4.44 us (8%)
    pallas_call x1, Pallas kernels, on_device(): pl.pallas_call(functools.partial(kernel, R, C, U, BS, SR), out_shape=jax....  53.2 us
    unnamed x12, local copies, waits for them, and re-layouts  2.4 us
    reshape x1, local copies, waits for them, and re-layouts, on_device(): return out.reshape(BS, 1, flat)  2.05 us

profile of v1, /device:TPU:2, one launch (start us, length us, event | category | flops | bytes accessed | tf_op | source)
XLA Modules:
  0.0 57.7 jit_solution(14011366205316346148)
XLA Ops:
  0.0 0.0 copy-start.4
  0.0 0.7 %copy-done.4 = f32[4,1,256]{2,1,0:T(1,128)S(1)} copy-done((f32[4,1,256]{2,1,0:T(1,128)S(1)}, f32[4,1,256]{2,1,0:T(1,128)}, u32[]{:S(2)}) %copy-start.4) | copy-done | bytes 4120
  0.7 0.0 copy-start
  0.7 0.0 copy-start.1
  0.7 0.0 copy-start.2
  0.7 0.0 copy-start.3
  0.7 1.6 %copy.12 = f32[256,1,1024]{2,0,1:T(8,128)S(1)} copy(f32[256,1,1024]{2,1,0:T(1,128)} %param.6) | data formatting | bytes 2097152
  2.3 0.0 copy-done
  2.3 0.1 copy-done.1
  2.4 0.0 copy-done.2
  2.4 0.0 copy-done.3
  2.4 53.2 %shard_map.64 = f32[256,1024]{1,0:T(8,128)S(1)} custom-call(f32[256,1024]{1,0:T(8,128)S(1)} %bitcast.12, bf16[256,1024]{1,0:T(8,128)(2,1)S(1)} %bitcast.14, bf16[2,256,1024]{2,1,0:T(8,128)(2,1)S(1)} %bitcast.13, f32[4,32,256]{2,1,0:T(8,128)S(1)} %bitcast.15, f32[4,32,256]{2,1,0:T(8,128)S(1)} %bitcast.16, f32[4,256]{1,0:T(4,128)S(1)} %bitcast.17), custom_call_target="tpu_custom_call" | custom-call | tf_op jit(solution)/shard_map/pallas_call | solution.py:317
  55.6 2.0 %copy.7 = f32[256,1,1024]{2,1,0:T(1,128)} copy(f32[256,1,1024]{2,0,1:T(8,128)S(1)} %bitcast.11) | data formatting | bytes 2097152 | tf_op jit(solution)/shard_map/reshape | solution.py:345
  (1 shorter events, 0.0 us)
Async XLA Ops:
  0.0 0.7 %copy-start.4 = (f32[4,1,256]{2,1,0:T(1,128)S(1)}, f32[4,1,256]{2,1,0:T(1,128)}, u32[]{:S(2)}) copy-start(f32[4,1,256]{2,1,0:T(1,128)} %param.11) | copy-start | bytes 12292
  0.7 1.6 %copy-start = (bf16[2,256,1,1024]{3,1,2,0:T(8,128)(2,1)S(1)}, bf16[2,256,1,1024]{3,1,2,0:T(8,128)(2,1)}, u32[]{:S(2)}) copy-start(bf16[2,256,1,1024]{3,1,2,0:T(8,128)(2,1)} %param.8) | copy-start | bytes 3145732
  0.7 1.7 %copy-start.1 = (bf16[256,1,1024]{2,0,1:T(8,128)(2,1)S(1)}, bf16[256,1,1024]{2,0,1:T(8,128)(2,1)}, u32[]{:S(2)}) copy-start(bf16[256,1,1024]{2,0,1:T(8,128)(2,1)} %param.7) | copy-start | bytes 1572868
  0.7 1.7 %copy-start.2 = (f32[4,1,32,256]{3,2,1,0:T(8,128)S(1)}, f32[4,1,32,256]{3,2,1,0:T(8,128)}, u32[]{:S(2)}) copy-start(f32[4,1,32,256]{3,2,1,0:T(8,128)} %param.9) | copy-start | bytes 393220
  0.7 1.7 %copy-start.3 = (f32[4,1,32,256]{3,2,1,0:T(8,128)S(1)}, f32[4,1,32,256]{3,2,1,0:T(8,128)}, u32[]{:S(2)}) copy-start(f32[4,1,32,256]{3,2,1,0:T(8,128)} %param.10) | copy-start | bytes 393220

commit v2 on v1

v2 whole, which is shorter than its diff:
```python
import functools

import jax
import jax.numpy as jnp
from jax import lax
from jax.experimental import pallas as pl
from jax.experimental.pallas import tpu as pltpu
from jax.sharding import PartitionSpec as P

STEPS = 2
PARTS = 2
PAD = 16
OP_MAX = 1.3
MESH = pl.DeviceIdType.MESH
F32 = jnp.float32
BF16 = jnp.bfloat16
NN = (((1,), (0,)), ((), ()))
NT = (((1,), (1,)), ((), ()))
scope = jax.named_scope


def halves(x):
    hi = x.astype(BF16)
    return hi, (x - hi.astype(F32)).astype(BF16)


def mm(a, b, dims):
    return lax.dot_general(a, b, dims, preferred_element_type=F32)


def dot3(a, b, dims):
    ah, al = halves(a)
    bh, bl = halves(b)
    return mm(ah, bh, dims) + (mm(ah, bl, dims) + mm(al, bh, dims))


def encode(x, inverse):
    v = jnp.exp2(jnp.sqrt(jnp.abs(x) * inverse) * 250.0 - 125.0)
    return jnp.where(x < 0, -v, v).astype(BF16)


def decode(v, scale):
    v = v.astype(F32)
    y = jnp.log2(jnp.abs(v)) * (1.0 / 250.0) + 0.5
    x = y * y * scale
    return jnp.where(v < 0, -x, x)


def kernel(R, C, U, BS, SR, state, upper_in, lower_in, factor, cofactor, rates_in, out,
           upper, lower, raw, rates, enc, ops, mats, ebuf, xz, own, atb, an,
           load_sem, ops_sem, e_sem, xz_sem, at_sem, an_sem, send_sem):
    H = R // 2
    r = lax.axis_index("row")
    c = lax.axis_index("col")
    d = [2 * R - 1 - s for s in range(STEPS)]

    def owner(row, s):
        return (d[s] - row) % C

    o = [owner(r, s) for s in range(STEPS)]
    sends = []
    me = r * C + c

    barrier = pltpu.get_barrier_semaphore()

    @pl.loop(1, R * C)
    def _(k):
        peer = (me + k) % (R * C)
        pl.semaphore_signal(barrier, inc=1, device_id=(peer // C, peer % C), device_id_type=MESH)

    pltpu.make_async_copy(cofactor, raw.at[0], load_sem.at[0]).start()
    pltpu.make_async_copy(factor, raw.at[1], load_sem.at[0]).start()
    pltpu.make_async_copy(rates_in.at[:, 0, :], rates, load_sem.at[1]).start()
    pltpu.make_async_copy(lower_in.at[0], lower, load_sem.at[2]).start()
    lanes = out.shape[1] // state.shape[1]
    for j in range(state.shape[1]):
        pltpu.make_async_copy(state.at[:, j, 0, :], out.at[:, pl.ds(j * lanes, lanes)], load_sem.at[3]).start()
    pltpu.make_async_copy(upper_in, upper, load_sem.at[4]).start()

    def arrive(ref, sem):
        pltpu.make_async_copy(ref, ref, sem).wait()

    def send(cond, src, dst, sem, dev):
        copy = pltpu.make_async_remote_copy(
            src_ref=src, dst_ref=dst, send_sem=send_sem.at[0], recv_sem=sem,
            device_id=dev, device_id_type=MESH)
        sends.append((cond, copy))

        @pl.when(cond)
        def _():
            copy.start()

    def send_or_local(cond, src, dst, sem, dev):
        mine = (dev[0] == r) & (dev[1] == c)
        send(cond & jnp.logical_not(mine), src, dst, sem, dev)

        @pl.when(cond & mine)
        def _():
            pltpu.make_async_copy(src, dst, sem).start()

    def slot(u):
        if isinstance(u, int):
            return pl.ds(u * BS, BS)
        return pl.ds(pl.multiple_of(u * BS, BS), BS)

    def target(row, m, s):
        return (row <= m) & (row + m < d[s])

    with scope("encode"):
        arrive(raw, load_sem.at[0])
        for u in range(U):
            both = jnp.concatenate([raw[0, u], raw[1, u]], axis=0)
            enc[u] = encode(both, 1.0 / OP_MAX)
        arrive(rates, load_sem.at[1])

    with scope("barrier"):
        pl.semaphore_wait(barrier, R * C - 1)

    def send_operators(s):
        for u in range(U):
            m = c + C * u
            if u >= U // 2 - s:
                to = d[s] - m
                send_or_local((to >= 0) & (to < R), enc.at[u], ops.at[1, r], ops_sem.at[1], (to, c))
            if u < U // 2:
                send_or_local(m < R, enc.at[u], ops.at[0, r], ops_sem.at[0], (m, owner(m, s)))

    def send_lower():
        to = (r + H) % R
        for u in range(U - 1, -1, -1):
            m = c + C * u
            send(target(to, m, 0) & (m != to), lower.at[:, slot(u)], atb.at[0, u], at_sem.at[0, u], (to, c))

    def send_upper(cond):
        for u in range(U):
            m = c + C * u - 1
            to = (c + C - 1) % C
            to_u = jnp.maximum(jnp.where(c >= 1, u, u - 1), 0)
            send(cond & (m >= 0) & target(r, m, 1), upper.at[:, slot(u)], an.at[to_u],
                 an_sem.at[to_u], (r, to))

    def hand_down(u):
        m = c + C * u
        live = (r >= 1) & (m >= r) & target(r - 1, m, 1)
        to = (jnp.maximum(r - 1, 0), c)
        if u < U // 2:
            send(live & (m == r), upper.at[:, slot(u)], atb.at[1, u], at_sem.at[1, u], to)
        send(live & (m != r), atb.at[0, u], atb.at[1, u], at_sem.at[1, u], to)

    with scope("sends0"):
        send_operators(0)
        for s in range(STEPS):
            send_or_local(c == r % C, rates, ebuf, e_sem.at[0], (r, o[s]))
        arrive(lower, load_sem.at[2])
        send_lower()
        send_operators(1)
        arrive(upper, load_sem.at[4])
        arrive(out, load_sem.at[3])
        send_upper((c != o[0]) & (c != o[1]))

    half = BS // PARTS

    def part(h):
        if h == 0:
            return pl.ds(0, PAD + half)
        return pl.ds(PAD + h * half, half)

    def spread(s, h, who):
        own_col = r % C == c
        k = jnp.where(own_col, r // C, (d[s] - r) // C)
        has = (own_col | (c == o[s])) & who

        def give(cond, to):
            send(cond & has, xz.at[s, U, part(h)], xz.at[s, k, part(h)], xz_sem.at[s, k, h], (to, c))

        give(r % 2 == 1, jnp.maximum(r - 1, 0))
        for back in range(1, R // 2):
            pair = r // 2 - back
            give(pair >= 0, jnp.maximum(2 * pair + 1 - r % 2, 0))

    def give_row(s):
        at = c == o[s]
        far = (o[s] == 0) & at
        for h in range(PARTS):
            block = xz.at[s, U, part(h)]
            sem = xz_sem.at[s, U, h]
            if s == 0:
                send(far, block, block, sem, (r, C - 1))
                send(at & (o[s] >= 1), block, block, sem, (r, jnp.maximum(c - 1, 0)))
                spread(s, h, at)
                send(at & (o[s] >= 2), block, block, sem, (r, jnp.maximum(c - 2, 0)))
                send(at & (o[s] <= C - 3) & jnp.logical_not(far & (C == 3)), block, block, sem, (r, jnp.minimum(c + 2, C - 1)))
                send(at & (o[s] <= C - 2), block, block, sem, (r, jnp.minimum(c + 1, C - 1)))
            else:
                send(at & (o[s] >= 2), block, block, sem, (r, jnp.maximum(c - 2, 0)))
                send(at & (o[s] <= C - 3), block, block, sem, (r, jnp.minimum(c + 2, C - 1)))
                spread(s, h, at)
                send(at & (o[s] >= 1), block, block, sem, (r, jnp.maximum(c - 1, 0)))
                send(at & (o[s] <= C - 2), block, block, sem, (r, jnp.minimum(c + 1, C - 1)))

    def take_row(s):
        other = c != o[s]
        down = (c <= o[s] - 2) & (c >= 1)
        up = (c >= o[s] + 2) & (c < C - 1)
        if s == 0:
            up = up & jnp.logical_not((o[s] == 0) & (c == C - 2))
        for h in range(PARTS):
            block = xz.at[s, U, part(h)]
            sem = xz_sem.at[s, U, h]

            @pl.when(other)
            def _(block=block, sem=sem):
                arrive(block, sem)

            send(down, block, block, sem, (r, jnp.maximum(c - 1, 0)))
            send(up, block, block, sem, (r, jnp.minimum(c + 1, C - 1)))
            spread(s, h, other)

    def decoded(s, k):
        return decode(xz[s, k, PAD:], xz[s, k, 0:1, :].astype(F32))

    def split_own(s):
        xh, xl = halves(decoded(s, U))
        own[0] = xh
        own[1] = xl

    def solve(s):
        q = (d[s] - r) // C
        with scope("w_e"):
            arrive(ebuf, e_sem.at[0])
        left_e = jnp.transpose(jnp.broadcast_to(ebuf[pl.ds(r // C, 1), :], (BS, BS)))
        rate = left_e + rates[pl.ds(q, 1), :]
        for side in range(2):
            with scope("w_op%d" % side):
                arrive(ops.at[side], ops_sem.at[side])
            for k in range(R):
                both = decode(ops[side, k], OP_MAX)
                mats[2 * side, k * SR:(k + 1) * SR] = both[:SR]
                mats[2 * side + 1, k * SR:(k + 1) * SR] = both[SR:]
        mid = dot3(mats[0], out[:, slot(q)], NN)
        mid = dot3(mid, mats[2], NT) / rate
        mid = dot3(mats[1], mid, NN)
        x = -dot3(mid, mats[3], NT)
        out[:, slot(q)] = x
        peak = jnp.max(jnp.abs(x), axis=0, keepdims=True) * 1.01 + 1e-30
        scale = peak.astype(BF16)
        xz[s, U, :PAD] = jnp.broadcast_to(scale, (PAD, BS))
        xz[s, U, PAD:] = encode(x, 1.0 / scale.astype(F32))

    def z_index(u, s):
        m = c + C * u
        j = jnp.where(d[s] - m <= m, d[s] - m, m)
        k = jnp.where(j == r, U, jnp.where(j % C == c, j // C, u))
        return j, k

    def collect(u, s, extra=True):
        j, k = z_index(u, s)
        landed = r < j
        if u >= U // 2:
            landed = landed & (j % C != c)
        landed = landed & extra

        for h in range(PARTS):
            block = xz.at[s, u, part(h)]

            @pl.when(landed)
            def _(block=block, h=h):
                arrive(block, xz_sem.at[s, u, h])

            send(landed & (r // 2 < j // 2) & (r % 2 != j % 2), block, block,
                 xz_sem.at[s, u, h], (r + 1 - 2 * (r % 2), c))

    def right(u, s):
        m = c + C * u

        def apply(a, dims):
            out[:, slot(u)] -= mm(own[0], a, dims) + mm(own[1], a, dims)

        def moved():
            arrive(atb.at[s, u], at_sem.at[s, u])

        if u >= U // 2:
            moved()
            apply(atb[s, u], NN)
            return
        if s == 0:
            @pl.when(m == r)
            def _():
                apply(upper[:, slot(u)], NT)

            @pl.when(m != r)
            def _():
                moved()
                apply(atb[s, u], NN)
        else:
            @pl.when(m == r)
            def _():
                apply(an[u], NT)

            @pl.when(m == r + 1)
            def _():
                moved()
                apply(atb[s, u], NT)

            @pl.when(m > r + 1)
            def _():
                moved()
                apply(atb[s, u], NN)

    def left(u, s):
        j, k = z_index(u, s)
        a = an[u] if s > 0 else upper[:, slot(u)]
        zh, zl = halves(decoded(s, k))

        def apply(dims):
            out[:, slot(u)] -= mm(a, zh, dims) + mm(a, zl, dims)

        low, high = C * u, C * u + C - 1
        if 2 * low >= d[s]:
            apply(NN)
        elif 2 * high < d[s]:
            apply(NT)
        else:
            m = c + C * u
            straight = d[s] - m <= m
            pl.when(straight)(lambda: apply(NN))
            pl.when(jnp.logical_not(straight))(lambda: apply(NT))

    def on_targets(s, fns, but=None):
        for u in range(U):
            live = target(r, c + C * u, s)
            if but is not None:
                live = live & jnp.logical_not(but(u))

            @pl.when(live)
            def _(u=u):
                for fn in fns:
                    fn(u, s)

    @pl.when(c == o[0])
    def _():
        with scope("solve0"):
            solve(0)

    with scope("give0"):
        give_row(0)
    with scope("take0"):
        take_row(0)
        split_own(0)
        send_upper(c == o[0])

    q1 = (d[1] - r) // C
    first = c == o[1]

    def picked(u):
        return first & (q1 == u)

    with scope("pick0"):
        for u in range(U // 2 - 1, U):
            collect(u, 0, picked(u))

            @pl.when(picked(u))
            def _(u=u):
                right(u, 0)
                left(u, 0)

    @pl.when(first)
    def _():
        with scope("solve1"):
            solve(1)

    with scope("give1"):
        give_row(1)
        send_upper(c == o[1])

    with scope("right0"):
        on_targets(0, (right,), picked)
    with scope("hand"):
        for u in range(U):
            hand_down(u)
    with scope("collect0"):
        for u in range(U):
            collect(u, 0, jnp.logical_not(picked(u)))
    with scope("left0"):
        on_targets(0, (left,), picked)

    with scope("take1"):
        take_row(1)
        split_own(1)
    with scope("w_an"):
        for u in range(U):
            @pl.when(target(r, c + C * u, 1))
            def _(u=u):
                arrive(an.at[u], an_sem.at[u])
    with scope("right1"):
        on_targets(1, (right,))
    with scope("collect1"):
        for u in range(U):
            collect(u, 1)
    with scope("left1"):
        on_targets(1, (left,))

    with scope("drain"):
        for cond, copy in sends:
            @pl.when(cond)
            def _(copy=copy):
                copy.wait_send()


def store(work, out, sem):
    lanes = work.shape[1] // out.shape[1]
    for j in range(out.shape[1]):
        pltpu.make_async_copy(work.at[:, pl.ds(j * lanes, lanes)], out.at[:, j, 0, :], sem.at[0]).start()
    pltpu.make_async_copy(work, work, sem.at[0]).wait()


def on_device(state, coupling, coupling_t, factor, cofactor, rates):
    R = lax.axis_size("row")
    C = lax.axis_size("col")
    U = 2 * R // C
    BS = state.shape[0]
    SR = factor.shape[2]
    flat = U * BS
    lanes = 128
    vmem = pl.BlockSpec(memory_space=pltpu.VMEM)
    hbm = pl.BlockSpec(memory_space=pltpu.HBM)
    dma = pltpu.SemaphoreType.DMA
    work = pl.pallas_call(
        functools.partial(kernel, R, C, U, BS, SR),
        out_shape=jax.ShapeDtypeStruct((BS, flat), F32),
        in_specs=[hbm] * 6,
        out_specs=vmem,
        scratch_shapes=[
            pltpu.VMEM((BS, flat), BF16),
            pltpu.VMEM((BS, flat), BF16),
            pltpu.VMEM((2, U, SR, BS), F32),
            pltpu.VMEM((U, BS), F32),
            pltpu.VMEM((U, 2 * SR, BS), BF16),
            pltpu.VMEM((2, R, 2 * SR, BS), BF16),
            pltpu.VMEM((4, BS, BS), F32),
            pltpu.VMEM((U, BS), F32),
            pltpu.VMEM((STEPS, U + 1, PAD + BS, BS), BF16),
            pltpu.VMEM((2, BS, BS), BF16),
            pltpu.VMEM((STEPS, U, BS, BS), BF16),
            pltpu.VMEM((U, BS, BS), BF16),
            dma((5,)),
            dma((2,)),
            dma((1,)),
            dma((STEPS, U + 1, PARTS)),
            dma((STEPS, U)),
            dma((U,)),
            dma((1,)),
        ],
        compiler_params=pltpu.CompilerParams(
            collective_id=0, has_side_effects=True, vmem_limit_bytes=VMEM_LIMIT),
    )(
        state.reshape(BS, flat // lanes, 1, lanes),
        coupling.reshape(BS, flat),
        coupling_t.reshape(coupling_t.shape[0], BS, flat),
        factor.reshape(U, SR, BS),
        cofactor.reshape(U, SR, BS),
        rates,
    )
    out = pl.pallas_call(
        store,
        out_shape=jax.ShapeDtypeStruct((BS, flat // lanes, 1, lanes), F32),
        in_specs=[vmem],
        out_specs=hbm,
        scratch_shapes=[dma((1,))],
        compiler_params=pltpu.CompilerParams(vmem_limit_bytes=2 * 1024 * 1024),
    )(work)
    return out.reshape(BS, 1, flat)


VMEM_LIMIT = 61 * 1024 * 1024


def solution(mesh):
    return jax.shard_map(
        on_device,
        mesh=mesh,
        in_specs=(
            P("row", "col", None),
            P("row", "col", None),
            P(None, "row", "col", None),
            P(None, "col", "row", None),
            P(None, "col", "row", None),
            P(None, "col", None),
        ),
        out_specs=P("row", "col", None),
        check_vma=False,
    )
```

time: 57.8 us -> 45.8 us (0.79)
  the two profiles are of different devices: /device:TPU:2 before, /device:TPU:9 now
where the time goes in v2:
time: 45.8 us; the launch traced here: 45.7 us
  Pallas kernels  44.4 us (97%)
  local copies, waits for them, and re-layouts  1.22 us (3%)
    pallas_call x1, Pallas kernels, on_device(): pl.pallas_call(functools.partial(kernel, R, C, U, BS, SR), out_shape=jax....  43.5 us
    unnamed x2, local copies, waits for them, and re-layouts  1.22 us
    pallas_call x1, Pallas kernels, on_device(): pl.pallas_call(store, out_shape=jax.ShapeDtypeStruct((BS, flat // lanes,...  0.96 us

profile of v2, /device:TPU:9, one launch (start us, length us, event | category | flops | bytes accessed | tf_op | source)
XLA Modules:
  0.0 45.7 jit_solution(5407301422199546165)
XLA Ops:
  0.0 43.5 %shard_map.64.work = f32[256,1024]{1,0:T(8,128)} custom-call(f32[256,8,1,128]{3,2,1,0:T(1,128)} %bitcast.6, bf16[256,1024]{1,0:T(8,128)(2,1)} %bitcast.8, bf16[2,256,1024]{2,1,0:T(8,128)(2,1)} %bitcast.7, f32[4,32,256]{2,1,0:T(8,128)} %bitcast.9, f32[4,32,256]{2,1,0:T(8,128)} %bitcast.10, f32[4,1,256]{2,1,0:T(1,128)} %rates_in.1), custom_call_target="tpu_custom_call" | custom-call | tf_op jit(solution)/shard_map/pallas_call | solution.py:428
  43.5 0.0 copy-start
  43.5 1.2 %copy-done = f32[256,1024]{1,0:T(8,128)S(1)} copy-done((f32[256,1024]{1,0:T(8,128)S(1)}, f32[256,1024]{1,0:T(8,128)}, u32[]{:S(2)}) %copy-start) | copy-done | bytes 1048600
  44.7 1.0 %shard_map.65 = f32[256,8,1,128]{3,2,1,0:T(1,128)} custom-call(f32[256,1024]{1,0:T(8,128)S(1)} %copy-done), custom_call_target="tpu_custom_call" | custom-call | tf_op jit(solution)/shard_map/pallas_call | solution.py:464
Async XLA Ops:
  43.5 1.2 %copy-start = (f32[256,1024]{1,0:T(8,128)S(1)}, f32[256,1024]{1,0:T(8,128)}, u32[]{:S(2)}) copy-start(f32[256,1024]{1,0:T(8,128)} %shard_map.64.work) | copy-start | bytes 3145732

commit v3 on v2

--- a/solution.py
+++ b/solution.py
@@ -116,27 +116,33 @@
     with scope("barrier"):
         pl.semaphore_wait(barrier, R * C - 1)
 
-    def send_operators(s):
-        for u in range(U):
+    def send_left():
+        for u in range(U // 2):
             m = c + C * u
-            if u >= U // 2 - s:
-                to = d[s] - m
-                send_or_local((to >= 0) & (to < R), enc.at[u], ops.at[1, r], ops_sem.at[1], (to, c))
-            if u < U // 2:
-                send_or_local(m < R, enc.at[u], ops.at[0, r], ops_sem.at[0], (m, owner(m, s)))
-
-    def send_lower():
+            send_or_local(m < R, enc.at[u], ops.at[0, r], ops_sem.at[0], (m, owner(m, 0)))
+
+    def send_right(s):
+        for u in range(U // 2 - s, U):
+            to = d[s] - (c + C * u)
+            send_or_local((to >= 0) & (to < R), enc.at[u], ops.at[1, r], ops_sem.at[1], (to, c))
+
+    def send_lower(first):
         to = (r + H) % R
+        top = (d[0] - 1 - to - c) // C
         for u in range(U - 1, -1, -1):
             m = c + C * u
-            send(target(to, m, 0) & (m != to), lower.at[:, slot(u)], atb.at[0, u], at_sem.at[0, u], (to, c))
+            turn = u == top if first else u != top
+            send(target(to, m, 0) & (m != to) & turn, lower.at[:, slot(u)], atb.at[0, u], at_sem.at[0, u], (to, c))
+
+    early = (c >= 1) & (c != o[0]) & (c != o[1])
+    lowest = (jnp.maximum(r + 1 - c, 0) + C - 1) // C
 
     def send_upper(cond):
         for u in range(U):
             m = c + C * u - 1
             to = (c + C - 1) % C
             to_u = jnp.maximum(jnp.where(c >= 1, u, u - 1), 0)
-            send(cond & (m >= 0) & target(r, m, 1), upper.at[:, slot(u)], an.at[to_u],
+            send(cond(u) & (m >= 0) & target(r, m, 1), upper.at[:, slot(u)], an.at[to_u],
                  an_sem.at[to_u], (r, to))
 
     def hand_down(u):
@@ -148,15 +154,17 @@
         send(live & (m != r), atb.at[0, u], atb.at[1, u], at_sem.at[1, u], to)
 
     with scope("sends0"):
-        send_operators(0)
+        send_left()
+        send_right(0)
         for s in range(STEPS):
             send_or_local(c == r % C, rates, ebuf, e_sem.at[0], (r, o[s]))
         arrive(lower, load_sem.at[2])
-        send_lower()
-        send_operators(1)
+        send_lower(True)
+        send_right(1)
+        send_lower(False)
         arrive(upper, load_sem.at[4])
         arrive(out, load_sem.at[3])
-        send_upper((c != o[0]) & (c != o[1]))
+        send_upper(lambda u: early & (u == lowest))
 
     half = BS // PARTS
 
@@ -188,8 +196,6 @@
                 send(far, block, block, sem, (r, C - 1))
                 send(at & (o[s] >= 1), block, block, sem, (r, jnp.maximum(c - 1, 0)))
                 spread(s, h, at)
-                send(at & (o[s] >= 2), block, block, sem, (r, jnp.maximum(c - 2, 0)))
-                send(at & (o[s] <= C - 3) & jnp.logical_not(far & (C == 3)), block, block, sem, (r, jnp.minimum(c + 2, C - 1)))
                 send(at & (o[s] <= C - 2), block, block, sem, (r, jnp.minimum(c + 1, C - 1)))
             else:
                 send(at & (o[s] >= 2), block, block, sem, (r, jnp.maximum(c - 2, 0)))
@@ -200,8 +206,9 @@
 
     def take_row(s):
         other = c != o[s]
-        down = (c <= o[s] - 2) & (c >= 1)
-        up = (c >= o[s] + 2) & (c < C - 1)
+        near = 1 if s == 0 else 2
+        down = (c <= o[s] - near) & (c >= 1)
+        up = (c >= o[s] + near) & (c < C - 1)
         if s == 0:
             up = up & jnp.logical_not((o[s] == 0) & (c == C - 2))
         for h in range(PARTS):
@@ -233,6 +240,8 @@
         for side in range(2):
             with scope("w_op%d" % side):
                 arrive(ops.at[side], ops_sem.at[side])
+            if s == 0 and side == 0:
+                pass_left.start()
             for k in range(R):
                 both = decode(ops[side, k], OP_MAX)
                 mats[2 * side, k * SR:(k + 1) * SR] = both[:SR]
@@ -337,6 +346,11 @@
                 for fn in fns:
                     fn(u, s)
 
+    pass_left = pltpu.make_async_remote_copy(
+        src_ref=ops.at[0], dst_ref=ops.at[0], send_sem=send_sem.at[0], recv_sem=ops_sem.at[0],
+        device_id=(r, o[1]), device_id_type=MESH)
+    sends.append((c == o[0], pass_left))
+
     @pl.when(c == o[0])
     def _():
         with scope("solve0"):
@@ -347,7 +361,7 @@
     with scope("take0"):
         take_row(0)
         split_own(0)
-        send_upper(c == o[0])
+        send_upper(lambda u: (c != o[1]) & jnp.logical_not(early & (u == lowest)))
 
     q1 = (d[1] - r) // C
     first = c == o[1]
@@ -371,7 +385,7 @@
 
     with scope("give1"):
         give_row(1)
-        send_upper(c == o[1])
+        send_upper(lambda u: c == o[1])
 
     with scope("right0"):
         on_targets(0, (right,), picked)
@@ -394,11 +408,14 @@
                 arrive(an.at[u], an_sem.at[u])
     with scope("right1"):
         on_targets(1, (right,))
-    with scope("collect1"):
-        for u in range(U):
+    for u in range(U):
+        with scope("collect1_%d" % u):
             collect(u, 1)
-    with scope("left1"):
-        on_targets(1, (left,))
+
+        @pl.when(target(r, c + C * u, 1))
+        def _(u=u):
+            with scope("left1_%d" % u):
+                left(u, 1)
 
     with scope("drain"):
         for cond, copy in sends:
@@ -427,7 +444,7 @@
     dma = pltpu.SemaphoreType.DMA
     work = pl.pallas_call(
         functools.partial(kernel, R, C, U, BS, SR),
-        out_shape=jax.ShapeDtypeStruct((BS, flat), F32),
+        out_shape=pltpu.VMEM((BS, flat), F32),
         in_specs=[hbm] * 6,
         out_specs=vmem,
         scratch_shapes=[

time: 45.8 us -> 39.6 us (0.86)
  the two profiles are of different devices: /device:TPU:9 before, /device:TPU:0 now
where the time goes in v3:
time: 39.6 us; the launch traced here: 39.5 us
  Pallas kernels  39.5 us (100%)
    pallas_call x1, Pallas kernels, on_device(): pl.pallas_call(functools.partial(kernel, R, C, U, BS, SR), out_shape=pltp...  38.5 us
    pallas_call x1, Pallas kernels, on_device(): pl.pallas_call(store, out_shape=jax.ShapeDtypeStruct((BS, flat // lanes,...  0.97 us

profile of v3, /device:TPU:0, one launch (start us, length us, event | category | flops | bytes accessed | tf_op | source)
XLA Modules:
  0.0 39.5 jit_solution(15179615010716900421)
XLA Ops:
  0.0 38.5 %shard_map.64.work = f32[256,1024]{1,0:T(8,128)S(1)} custom-call(f32[256,8,1,128]{3,2,1,0:T(1,128)} %bitcast.6, bf16[256,1024]{1,0:T(8,128)(2,1)} %bitcast.8, bf16[2,256,1024]{2,1,0:T(8,128)(2,1)} %bitcast.7, f32[4,32,256]{2,1,0:T(8,128)} %bitcast.9, f32[4,32,256]{2,1,0:T(8,128)} %bitcast.10, f32[4,1,256]{2,1,0:T(1,128)} %rates_in.1), custom_call_target="tpu_custom_call" | custom-call | tf_op jit(solution)/shard_map/pallas_call | solution.py:445
  38.5 1.0 %shard_map.65 = f32[256,8,1,128]{3,2,1,0:T(1,128)} custom-call(f32[256,1024]{1,0:T(8,128)S(1)} %shard_map.64.work), custom_call_target="tpu_custom_call" | custom-call | tf_op jit(solution)/shard_map/pallas_call | solution.py:481

commit v4 on v3

--- a/solution.py
+++ b/solution.py
@@ -10,6 +10,7 @@
 STEPS = 2
 PARTS = 2
 PAD = 16
+SAME = False
 OP_MAX = 1.3
 MESH = pl.DeviceIdType.MESH
 F32 = jnp.float32
@@ -29,9 +30,7 @@
 
 
 def dot3(a, b, dims):
-    ah, al = halves(a)
-    bh, bl = halves(b)
-    return mm(ah, bh, dims) + (mm(ah, bl, dims) + mm(al, bh, dims))
+    return mm(a[0], b[0], dims) + (mm(a[0], b[1], dims) + mm(a[1], b[0], dims))
 
 
 def encode(x, inverse):
@@ -47,7 +46,7 @@
 
 
 def kernel(R, C, U, BS, SR, state, upper_in, lower_in, factor, cofactor, rates_in, out,
-           upper, lower, raw, rates, enc, ops, mats, ebuf, xz, own, atb, an,
+           upper, lower, turned, raw, rates, enc, ops, mats, ebuf, xz, own, atb, an,
            load_sem, ops_sem, e_sem, xz_sem, at_sem, an_sem, send_sem):
     H = R // 2
     r = lax.axis_index("row")
@@ -71,7 +70,7 @@
     pltpu.make_async_copy(cofactor, raw.at[0], load_sem.at[0]).start()
     pltpu.make_async_copy(factor, raw.at[1], load_sem.at[0]).start()
     pltpu.make_async_copy(rates_in.at[:, 0, :], rates, load_sem.at[1]).start()
-    pltpu.make_async_copy(lower_in.at[0], lower, load_sem.at[2]).start()
+    pltpu.make_async_copy(lower_in, lower, load_sem.at[2]).start()
     lanes = out.shape[1] // state.shape[1]
     for j in range(state.shape[1]):
         pltpu.make_async_copy(state.at[:, j, 0, :], out.at[:, pl.ds(j * lanes, lanes)], load_sem.at[3]).start()
@@ -116,10 +115,10 @@
     with scope("barrier"):
         pl.semaphore_wait(barrier, R * C - 1)
 
-    def send_left():
+    def send_left(s):
         for u in range(U // 2):
             m = c + C * u
-            send_or_local(m < R, enc.at[u], ops.at[0, r], ops_sem.at[0], (m, owner(m, 0)))
+            send_or_local(m < R, enc.at[u], ops.at[0, r], ops_sem.at[0], (m, owner(m, s)))
 
     def send_right(s):
         for u in range(U // 2 - s, U):
@@ -132,17 +131,49 @@
         for u in range(U - 1, -1, -1):
             m = c + C * u
             turn = u == top if first else u != top
-            send(target(to, m, 0) & (m != to) & turn, lower.at[:, slot(u)], atb.at[0, u], at_sem.at[0, u], (to, c))
-
-    early = (c >= 1) & (c != o[0]) & (c != o[1])
-    lowest = (jnp.maximum(r + 1 - c, 0) + C - 1) // C
+            send(target(to, m, 0) & (m != to) & turn, lower.at[0, :, slot(u)], atb.at[0, u], at_sem.at[0, u], (to, c))
+
+    q1 = (d[1] - r) // C
+    first = c == o[1]
+    top = (d[0] - 1 - r - c) // C
+    ahead = c != o[0]
+
+    def needs(u):
+        m = c + C * u
+        return target(r, m, 0) & (m != r)
+
+    def picked(u):
+        return first & (q1 == u)
+
+    def crossing(i, m):
+        return (m % C == C - 1) | ((m - i) % C == 0 if SAME else False)
+
+    def send_turned(cond):
+        for t in range(2):
+            m = (r + H) % R + R * t - 1
+            for u in range(U // 2):
+                i = c + C * u
+                live = cond & (m >= 0) & target(i, m, 1) & crossing(i, m)
+                to_u = jnp.clip(m // C, 0, U - 1)
+                mine = (i == r) & (m % C == c)
+                k = t * (U // 2) + u
+
+                @pl.when(live)
+                def _(t=t, u=u, k=k):
+                    turned[k] = jnp.transpose(lower[t, :, slot(u)])
+
+                send(live & jnp.logical_not(mine), turned.at[k], an.at[to_u], an_sem.at[to_u], (i, m % C))
+
+                @pl.when(live & mine)
+                def _(k=k, to_u=to_u):
+                    pltpu.make_async_copy(turned.at[k], an.at[to_u], an_sem.at[to_u]).start()
 
     def send_upper(cond):
         for u in range(U):
             m = c + C * u - 1
             to = (c + C - 1) % C
             to_u = jnp.maximum(jnp.where(c >= 1, u, u - 1), 0)
-            send(cond(u) & (m >= 0) & target(r, m, 1), upper.at[:, slot(u)], an.at[to_u],
+            send(cond & jnp.logical_not(crossing(r, m)) & (m >= 0) & target(r, m, 1), upper.at[:, slot(u)], an.at[to_u],
                  an_sem.at[to_u], (r, to))
 
     def hand_down(u):
@@ -154,17 +185,25 @@
         send(live & (m != r), atb.at[0, u], atb.at[1, u], at_sem.at[1, u], to)
 
     with scope("sends0"):
-        send_left()
+        send_left(0)
         send_right(0)
         for s in range(STEPS):
             send_or_local(c == r % C, rates, ebuf, e_sem.at[0], (r, o[s]))
+        send_left(1)
         arrive(lower, load_sem.at[2])
         send_lower(True)
         send_right(1)
         send_lower(False)
         arrive(upper, load_sem.at[4])
         arrive(out, load_sem.at[3])
-        send_upper(lambda u: early & (u == lowest))
+        send_upper(c != o[0])
+
+    with scope("gate"):
+        @pl.when(ahead & needs(top))
+        def _():
+            arrive(atb.at[0, top], at_sem.at[0, top])
+
+        send_turned(c != o[0])
 
     half = BS // PARTS
 
@@ -188,29 +227,24 @@
 
     def give_row(s):
         at = c == o[s]
-        far = (o[s] == 0) & at
+        goal = (o[s] + C - 1) % C
         for h in range(PARTS):
             block = xz.at[s, U, part(h)]
             sem = xz_sem.at[s, U, h]
             if s == 0:
-                send(far, block, block, sem, (r, C - 1))
-                send(at & (o[s] >= 1), block, block, sem, (r, jnp.maximum(c - 1, 0)))
+                send(at, block, block, sem, (r, goal))
                 spread(s, h, at)
-                send(at & (o[s] <= C - 2), block, block, sem, (r, jnp.minimum(c + 1, C - 1)))
-            else:
-                send(at & (o[s] >= 2), block, block, sem, (r, jnp.maximum(c - 2, 0)))
-                send(at & (o[s] <= C - 3), block, block, sem, (r, jnp.minimum(c + 2, C - 1)))
-                spread(s, h, at)
-                send(at & (o[s] >= 1), block, block, sem, (r, jnp.maximum(c - 1, 0)))
-                send(at & (o[s] <= C - 2), block, block, sem, (r, jnp.minimum(c + 1, C - 1)))
+            for far_by in range(C - 1, 0, -1):
+                for to in (c - far_by, c + far_by):
+                    live = at & (to >= 0) & (to < C)
+                    if s == 0:
+                        live = live & (to != goal)
+                    send(live, block, block, sem, (r, jnp.clip(to, 0, C - 1)))
+                if far_by == 2 and s == 1:
+                    spread(s, h, at)
 
     def take_row(s):
         other = c != o[s]
-        near = 1 if s == 0 else 2
-        down = (c <= o[s] - near) & (c >= 1)
-        up = (c >= o[s] + near) & (c < C - 1)
-        if s == 0:
-            up = up & jnp.logical_not((o[s] == 0) & (c == C - 2))
         for h in range(PARTS):
             block = xz.at[s, U, part(h)]
             sem = xz_sem.at[s, U, h]
@@ -219,8 +253,6 @@
             def _(block=block, sem=sem):
                 arrive(block, sem)
 
-            send(down, block, block, sem, (r, jnp.maximum(c - 1, 0)))
-            send(up, block, block, sem, (r, jnp.minimum(c + 1, C - 1)))
             spread(s, h, other)
 
     def decoded(s, k):
@@ -231,25 +263,30 @@
         own[0] = xh
         own[1] = xl
 
-    def solve(s):
-        q = (d[s] - r) // C
+    def prepare():
         with scope("w_e"):
             arrive(ebuf, e_sem.at[0])
-        left_e = jnp.transpose(jnp.broadcast_to(ebuf[pl.ds(r // C, 1), :], (BS, BS)))
-        rate = left_e + rates[pl.ds(q, 1), :]
+        group = max(1, 16 // SR)
         for side in range(2):
             with scope("w_op%d" % side):
                 arrive(ops.at[side], ops_sem.at[side])
-            if s == 0 and side == 0:
-                pass_left.start()
-            for k in range(R):
-                both = decode(ops[side, k], OP_MAX)
-                mats[2 * side, k * SR:(k + 1) * SR] = both[:SR]
-                mats[2 * side + 1, k * SR:(k + 1) * SR] = both[SR:]
-        mid = dot3(mats[0], out[:, slot(q)], NN)
-        mid = dot3(mid, mats[2], NT) / rate
-        mid = dot3(mats[1], mid, NN)
-        x = -dot3(mid, mats[3], NT)
+            for k in range(0, R, group):
+                both = [decode(ops[side, k + i], OP_MAX) for i in range(group)]
+                for which in range(2):
+                    rows = [b[which * SR:(which + 1) * SR] for b in both]
+                    hi, lo = halves(rows[0] if group == 1 else jnp.concatenate(rows, axis=0))
+                    mats[2 * side + which, 0, k * SR:(k + group) * SR] = hi
+                    mats[2 * side + which, 1, k * SR:(k + group) * SR] = lo
+
+    def solve(s):
+        q = (d[s] - r) // C
+        left_e = jnp.transpose(jnp.broadcast_to(ebuf[pl.ds(r // C, 1), :], (BS, BS)))
+        rate = left_e + rates[pl.ds(q, 1), :]
+        mat = [(mats[k, 0], mats[k, 1]) for k in range(4)]
+        mid = dot3(mat[0], halves(out[:, slot(q)]), NN)
+        mid = dot3(halves(mid), mat[2], NT) / rate
+        mid = dot3(mat[1], halves(mid), NN)
+        x = -dot3(halves(mid), mat[3], NT)
         out[:, slot(q)] = x
         peak = jnp.max(jnp.abs(x), axis=0, keepdims=True) * 1.01 + 1e-30
         scale = peak.astype(BF16)
@@ -286,7 +323,8 @@
             out[:, slot(u)] -= mm(own[0], a, dims) + mm(own[1], a, dims)
 
         def moved():
-            arrive(atb.at[s, u], at_sem.at[s, u])
+            if s > 0:
+                arrive(atb.at[s, u], at_sem.at[s, u])
 
         if u >= U // 2:
             moved()
@@ -346,28 +384,25 @@
                 for fn in fns:
                     fn(u, s)
 
-    pass_left = pltpu.make_async_remote_copy(
-        src_ref=ops.at[0], dst_ref=ops.at[0], send_sem=send_sem.at[0], recv_sem=ops_sem.at[0],
-        device_id=(r, o[1]), device_id_type=MESH)
-    sends.append((c == o[0], pass_left))
-
     @pl.when(c == o[0])
     def _():
         with scope("solve0"):
+            prepare()
             solve(0)
 
     with scope("give0"):
         give_row(0)
+        send_upper(c == o[0])
+        send_turned(c == o[0])
+
+    @pl.when(first)
+    def _():
+        with scope("prep"):
+            prepare()
+
     with scope("take0"):
         take_row(0)
         split_own(0)
-        send_upper(lambda u: (c != o[1]) & jnp.logical_not(early & (u == lowest)))
-
-    q1 = (d[1] - r) // C
-    first = c == o[1]
-
-    def picked(u):
-        return first & (q1 == u)
 
     with scope("pick0"):
         for u in range(U // 2 - 1, U):
@@ -385,13 +420,16 @@
 
     with scope("give1"):
         give_row(1)
-        send_upper(lambda u: c == o[1])
-
+
+    with scope("hand"):
+        for u in range(U):
+            @pl.when(needs(u) & jnp.logical_not(ahead & (top == u)))
+            def _(u=u):
+                arrive(atb.at[0, u], at_sem.at[0, u])
+
+            hand_down(u)
     with scope("right0"):
         on_targets(0, (right,), picked)
-    with scope("hand"):
-        for u in range(U):
-            hand_down(u)
     with scope("collect0"):
         for u in range(U):
             collect(u, 0, jnp.logical_not(picked(u)))
@@ -449,12 +487,13 @@
         out_specs=vmem,
         scratch_shapes=[
             pltpu.VMEM((BS, flat), BF16),
-            pltpu.VMEM((BS, flat), BF16),
+            pltpu.VMEM((2, BS, flat), BF16),
+            pltpu.VMEM((U, BS, BS), BF16),
             pltpu.VMEM((2, U, SR, BS), F32),
             pltpu.VMEM((U, BS), F32),
             pltpu.VMEM((U, 2 * SR, BS), BF16),
             pltpu.VMEM((2, R, 2 * SR, BS), BF16),
-            pltpu.VMEM((4, BS, BS), F32),
+            pltpu.VMEM((4, 2, BS, BS), BF16),
             pltpu.VMEM((U, BS), F32),
             pltpu.VMEM((STEPS, U + 1, PAD + BS, BS), BF16),
             pltpu.VMEM((2, BS, BS), BF16),

time: 39.6 us -> 35.9 us (0.907)
  the two profiles are of different devices: /device:TPU:0 before, /device:TPU:16 now
where the time goes in v4:
time: 35.9 us; the launch traced here: 35.8 us
  Pallas kernels  35.8 us (100%)
    pallas_call x1, Pallas kernels, on_device(): pl.pallas_call(functools.partial(kernel, R, C, U, BS, SR), out_shape=pltp...  34.8 us
    pallas_call x1, Pallas kernels, on_device(): pl.pallas_call(store, out_shape=jax.ShapeDtypeStruct((BS, flat // lanes,...  0.97 us

profile of v4, /device:TPU:16, one launch (start us, length us, event | category | flops | bytes accessed | tf_op | source)
XLA Modules:
  0.0 35.8 jit_solution(4876096145522278413)
XLA Ops:
  0.0 34.8 %shard_map.64.work = f32[256,1024]{1,0:T(8,128)S(1)} custom-call(f32[256,8,1,128]{3,2,1,0:T(1,128)} %bitcast.6, bf16[256,1024]{1,0:T(8,128)(2,1)} %bitcast.8, bf16[2,256,1024]{2,1,0:T(8,128)(2,1)} %bitcast.7, f32[4,32,256]{2,1,0:T(8,128)} %bitcast.9, f32[4,32,256]{2,1,0:T(8,128)} %bitcast.10, f32[4,1,256]{2,1,0:T(1,128)} %rates_in.1), custom_call_target="tpu_custom_call" | custom-call | tf_op jit(solution)/shard_map/pallas_call | solution.py:483
  34.8 1.0 %shard_map.65 = f32[256,8,1,128]{3,2,1,0:T(1,128)} custom-call(f32[256,1024]{1,0:T(8,128)S(1)} %shard_map.64.work), custom_call_target="tpu_custom_call" | custom-call | tf_op jit(solution)/shard_map/pallas_call | solution.py:520

commit v5 on v4

--- a/solution.py
+++ b/solution.py
@@ -10,7 +10,7 @@
 STEPS = 2
 PARTS = 2
 PAD = 16
-SAME = False
+SAME = True
 OP_MAX = 1.3
 MESH = pl.DeviceIdType.MESH
 F32 = jnp.float32
@@ -123,7 +123,10 @@
     def send_right(s):
         for u in range(U // 2 - s, U):
             to = d[s] - (c + C * u)
-            send_or_local((to >= 0) & (to < R), enc.at[u], ops.at[1, r], ops_sem.at[1], (to, c))
+            live = (to >= 0) & (to < R)
+            if s > 0:
+                live = live & (to % 2 == 1)
+            send_or_local(live, enc.at[u], ops.at[1, r], ops_sem.at[1], (to, c))
 
     def send_lower(first):
         to = (r + H) % R
@@ -132,6 +135,12 @@
             m = c + C * u
             turn = u == top if first else u != top
             send(target(to, m, 0) & (m != to) & turn, lower.at[0, :, slot(u)], atb.at[0, u], at_sem.at[0, u], (to, c))
+
+    def send_middle():
+        for u in range(U):
+            m = c + C * u
+            send((r == 0) & (m >= H) & target(H - 1, m, 1), lower.at[0, :, slot(u)], atb.at[1, u],
+                 at_sem.at[1, u], (H - 1, c))
 
     q1 = (d[1] - r) // C
     first = c == o[1]
@@ -168,17 +177,24 @@
                 def _(k=k, to_u=to_u):
                     pltpu.make_async_copy(turned.at[k], an.at[to_u], an_sem.at[to_u]).start()
 
-    def send_upper(cond):
+    def send_upper(cond, held=None):
+        late = first & (r % 2 == 0)
         for u in range(U):
             m = c + C * u - 1
             to = (c + C - 1) % C
             to_u = jnp.maximum(jnp.where(c >= 1, u, u - 1), 0)
-            send(cond & jnp.logical_not(crossing(r, m)) & (m >= 0) & target(r, m, 1), upper.at[:, slot(u)], an.at[to_u],
+            if u >= U // 2:
+                now = late if held else cond & jnp.logical_not(late)
+            elif held:
+                continue
+            else:
+                now = cond
+            send(now & jnp.logical_not(crossing(r, m)) & (m >= 0) & target(r, m, 1), upper.at[:, slot(u)], an.at[to_u],
                  an_sem.at[to_u], (r, to))
 
-    def hand_down(u):
+    def hand_down(u, rows):
         m = c + C * u
-        live = (r >= 1) & (m >= r) & target(r - 1, m, 1)
+        live = rows & (r >= 1) & (r != H) & (m >= r) & target(r - 1, m, 1)
         to = (jnp.maximum(r - 1, 0), c)
         if u < U // 2:
             send(live & (m == r), upper.at[:, slot(u)], atb.at[1, u], at_sem.at[1, u], to)
@@ -194,6 +210,7 @@
         send_lower(True)
         send_right(1)
         send_lower(False)
+        send_middle()
         arrive(upper, load_sem.at[4])
         arrive(out, load_sem.at[3])
         send_upper(c != o[0])
@@ -225,29 +242,40 @@
             pair = r // 2 - back
             give(pair >= 0, jnp.maximum(2 * pair + 1 - r % 2, 0))
 
+    def wants(col, s):
+        return (col - r) % C < d[s] - 2 * r
+
     def give_row(s):
         at = c == o[s]
+        home = r % C
         goal = (o[s] + C - 1) % C
+        def give(cond, to):
+            for h in range(PARTS):
+                block = xz.at[s, U, part(h)]
+                send(at & cond, block, block, xz_sem.at[s, U, h], (r, jnp.clip(to, 0, C - 1)))
+
+        if s == 0:
+            give(True, goal)
+        else:
+            give(home != c, home)
+        for h in range(PARTS):
+            spread(s, h, at)
+        if s == 0:
+            give((home != goal) & (home != c), home)
+        for far_by in range(C - 1, 0, -1):
+            for to in (c - far_by, c + far_by):
+                live = (to >= 0) & (to < C) & (to != home) & wants(to, s)
+                if s == 0:
+                    live = live & (to != goal)
+                give(live, to)
+
+    def take_row(s):
+        other = (c != o[s]) & (wants(c, s) | (c == r % C))
+        if s == 0:
+            other = other | first
         for h in range(PARTS):
             block = xz.at[s, U, part(h)]
             sem = xz_sem.at[s, U, h]
-            if s == 0:
-                send(at, block, block, sem, (r, goal))
-                spread(s, h, at)
-            for far_by in range(C - 1, 0, -1):
-                for to in (c - far_by, c + far_by):
-                    live = at & (to >= 0) & (to < C)
-                    if s == 0:
-                        live = live & (to != goal)
-                    send(live, block, block, sem, (r, jnp.clip(to, 0, C - 1)))
-                if far_by == 2 and s == 1:
-                    spread(s, h, at)
-
-    def take_row(s):
-        other = c != o[s]
-        for h in range(PARTS):
-            block = xz.at[s, U, part(h)]
-            sem = xz_sem.at[s, U, h]
 
             @pl.when(other)
             def _(block=block, sem=sem):
@@ -260,16 +288,18 @@
 
     def split_own(s):
         xh, xl = halves(decoded(s, U))
-        own[0] = xh
-        own[1] = xl
-
-    def prepare():
+        own[s, 0] = xh
+        own[s, 1] = xl
+
+    def prepare(s):
         with scope("w_e"):
             arrive(ebuf, e_sem.at[0])
         group = max(1, 16 // SR)
         for side in range(2):
             with scope("w_op%d" % side):
                 arrive(ops.at[side], ops_sem.at[side])
+            if s == 0 and side == 1:
+                pl.when(r % 2 == 1)(hand_right.start)
             for k in range(0, R, group):
                 both = [decode(ops[side, k + i], OP_MAX) for i in range(group)]
                 for which in range(2):
@@ -299,9 +329,10 @@
         k = jnp.where(j == r, U, jnp.where(j % C == c, j // C, u))
         return j, k
 
-    def collect(u, s, extra=True):
+    def collect(u, s, direct, extra=True):
         j, k = z_index(u, s)
-        landed = r < j
+        crossed = (r // 2 < j // 2) & (r % 2 != j % 2)
+        landed = (r < j) & (crossed if direct else jnp.logical_not(crossed))
         if u >= U // 2:
             landed = landed & (j % C != c)
         landed = landed & extra
@@ -313,14 +344,14 @@
             def _(block=block, h=h):
                 arrive(block, xz_sem.at[s, u, h])
 
-            send(landed & (r // 2 < j // 2) & (r % 2 != j % 2), block, block,
-                 xz_sem.at[s, u, h], (r + 1 - 2 * (r % 2), c))
+            if direct:
+                send(landed, block, block, xz_sem.at[s, u, h], (r + 1 - 2 * (r % 2), c))
 
     def right(u, s):
         m = c + C * u
 
         def apply(a, dims):
-            out[:, slot(u)] -= mm(own[0], a, dims) + mm(own[1], a, dims)
+            out[:, slot(u)] -= mm(own[s, 0], a, dims) + mm(own[s, 1], a, dims)
 
         def moved():
             if s > 0:
@@ -330,29 +361,21 @@
             moved()
             apply(atb[s, u], NN)
             return
-        if s == 0:
-            @pl.when(m == r)
-            def _():
-                apply(upper[:, slot(u)], NT)
-
-            @pl.when(m != r)
-            def _():
-                moved()
-                apply(atb[s, u], NN)
-        else:
-            @pl.when(m == r)
-            def _():
-                apply(an[u], NT)
-
-            @pl.when(m == r + 1)
-            def _():
-                moved()
-                apply(atb[s, u], NT)
-
-            @pl.when(m > r + 1)
-            def _():
-                moved()
-                apply(atb[s, u], NN)
+        plain = (m == r + 1) & (r != H - 1) if s > 0 else m < r
+
+        @pl.when(m == r)
+        def _():
+            apply(upper[:, slot(u)] if s == 0 else an[u], NT)
+
+        @pl.when((m != r) & plain)
+        def _():
+            moved()
+            apply(atb[s, u], NT)
+
+        @pl.when((m != r) & jnp.logical_not(plain))
+        def _():
+            moved()
+            apply(atb[s, u], NN)
 
     def left(u, s):
         j, k = z_index(u, s)
@@ -384,10 +407,15 @@
                 for fn in fns:
                     fn(u, s)
 
+    hand_right = pltpu.make_async_remote_copy(
+        src_ref=ops.at[1], dst_ref=ops.at[1], send_sem=send_sem.at[0], recv_sem=ops_sem.at[1],
+        device_id=(jnp.maximum(r - 1, 0), c), device_id_type=MESH)
+    sends.append(((c == o[0]) & (r % 2 == 1), hand_right))
+
     @pl.when(c == o[0])
     def _():
         with scope("solve0"):
-            prepare()
+            prepare(0)
             solve(0)
 
     with scope("give0"):
@@ -398,15 +426,16 @@
     @pl.when(first)
     def _():
         with scope("prep"):
-            prepare()
+            prepare(1)
 
     with scope("take0"):
         take_row(0)
-        split_own(0)
+        pl.when(wants(c, 0) | first)(lambda: split_own(0))
 
     with scope("pick0"):
         for u in range(U // 2 - 1, U):
-            collect(u, 0, picked(u))
+            collect(u, 0, True, picked(u))
+            collect(u, 0, False, picked(u))
 
             @pl.when(picked(u))
             def _(u=u):
@@ -420,25 +449,36 @@
 
     with scope("give1"):
         give_row(1)
-
-    with scope("hand"):
-        for u in range(U):
-            @pl.when(needs(u) & jnp.logical_not(ahead & (top == u)))
-            def _(u=u):
-                arrive(atb.at[0, u], at_sem.at[0, u])
-
-            hand_down(u)
-    with scope("right0"):
-        on_targets(0, (right,), picked)
+        send_upper(None, True)
+
+    def use_lower(rows):
+        with scope("hand"):
+            for u in range(U):
+                @pl.when(rows & needs(u) & jnp.logical_not(ahead & (top == u)))
+                def _(u=u):
+                    arrive(atb.at[0, u], at_sem.at[0, u])
+
+                hand_down(u, rows)
+        with scope("right0"):
+            on_targets(0, (right,), lambda u: picked(u) | jnp.logical_not(rows))
+
+    with scope("direct0"):
+        for u in range(U):
+            collect(u, 0, True, jnp.logical_not(picked(u)))
+    use_lower(r >= 2)
     with scope("collect0"):
         for u in range(U):
-            collect(u, 0, jnp.logical_not(picked(u)))
+            collect(u, 0, False, jnp.logical_not(picked(u)))
     with scope("left0"):
         on_targets(0, (left,), picked)
 
     with scope("take1"):
         take_row(1)
-        split_own(1)
+        pl.when(wants(c, 1))(lambda: split_own(1))
+    with scope("direct1"):
+        for u in range(U):
+            collect(u, 1, True)
+    use_lower(r < 2)
     with scope("w_an"):
         for u in range(U):
             @pl.when(target(r, c + C * u, 1))
@@ -448,18 +488,21 @@
         on_targets(1, (right,))
     for u in range(U):
         with scope("collect1_%d" % u):
-            collect(u, 1)
+            collect(u, 1, False)
 
         @pl.when(target(r, c + C * u, 1))
         def _(u=u):
             with scope("left1_%d" % u):
                 left(u, 1)
 
-    with scope("drain"):
-        for cond, copy in sends:
+    def drain(some):
+        for cond, copy in some:
             @pl.when(cond)
             def _(copy=copy):
                 copy.wait_send()
+
+    with scope("drain"):
+        drain(sends)
 
 
 def store(work, out, sem):
@@ -496,7 +539,7 @@
             pltpu.VMEM((4, 2, BS, BS), BF16),
             pltpu.VMEM((U, BS), F32),
             pltpu.VMEM((STEPS, U + 1, PAD + BS, BS), BF16),
-            pltpu.VMEM((2, BS, BS), BF16),
+            pltpu.VMEM((STEPS, 2, BS, BS), BF16),
             pltpu.VMEM((STEPS, U, BS, BS), BF16),
             pltpu.VMEM((U, BS, BS), BF16),
             dma((5,)),

time: 35.9 us -> 33.7 us (0.939)
  the two profiles are of different devices: /device:TPU:16 before, /device:TPU:0 now
where the time goes in v5:
time: 33.7 us; the launch traced here: 33.6 us
  Pallas kernels  33.6 us (100%)
    pallas_call x1, Pallas kernels, on_device(): pl.pallas_call(functools.partial(kernel, R, C, U, BS, SR), out_shape=pltp...  32.6 us
    pallas_call x1, Pallas kernels, on_device(): pl.pallas_call(store, out_shape=jax.ShapeDtypeStruct((BS, flat // lanes,...  0.97 us

profile of v5, /device:TPU:0, one launch (start us, length us, event | category | flops | bytes accessed | tf_op | source)
XLA Modules:
  0.0 33.6 jit_solution(6950016629687508514)
XLA Ops:
  0.0 32.6 %shard_map.64.work = f32[256,1024]{1,0:T(8,128)S(1)} custom-call(f32[256,8,1,128]{3,2,1,0:T(1,128)} %bitcast.6, bf16[256,1024]{1,0:T(8,128)(2,1)} %bitcast.8, bf16[2,256,1024]{2,1,0:T(8,128)(2,1)} %bitcast.7, f32[4,32,256]{2,1,0:T(8,128)} %bitcast.9, f32[4,32,256]{2,1,0:T(8,128)} %bitcast.10, f32[4,1,256]{2,1,0:T(1,128)} %rates_in.1), custom_call_target="tpu_custom_call" | custom-call | tf_op jit(solution)/shard_map/pallas_call | solution.py:526
  32.6 1.0 %shard_map.65 = f32[256,8,1,128]{3,2,1,0:T(1,128)} custom-call(f32[256,1024]{1,0:T(8,128)S(1)} %shard_map.64.work), custom_call_target="tpu_custom_call" | custom-call | tf_op jit(solution)/shard_map/pallas_call | solution.py:563

commit v6 on v5

--- a/solution.py
+++ b/solution.py
@@ -10,7 +10,8 @@
 STEPS = 2
 PARTS = 2
 PAD = 16
-SAME = True
+SAME = 2
+HOME = False
 OP_MAX = 1.3
 MESH = pl.DeviceIdType.MESH
 F32 = jnp.float32
@@ -62,13 +63,14 @@
 
     barrier = pltpu.get_barrier_semaphore()
 
+    pltpu.make_async_copy(cofactor, raw.at[0], load_sem.at[0]).start()
+    pltpu.make_async_copy(factor, raw.at[1], load_sem.at[0]).start()
+
     @pl.loop(1, R * C)
     def _(k):
         peer = (me + k) % (R * C)
         pl.semaphore_signal(barrier, inc=1, device_id=(peer // C, peer % C), device_id_type=MESH)
 
-    pltpu.make_async_copy(cofactor, raw.at[0], load_sem.at[0]).start()
-    pltpu.make_async_copy(factor, raw.at[1], load_sem.at[0]).start()
     pltpu.make_async_copy(rates_in.at[:, 0, :], rates, load_sem.at[1]).start()
     pltpu.make_async_copy(lower_in, lower, load_sem.at[2]).start()
     lanes = out.shape[1] // state.shape[1]
@@ -155,7 +157,9 @@
         return first & (q1 == u)
 
     def crossing(i, m):
-        return (m % C == C - 1) | ((m - i) % C == 0 if SAME else False)
+        beside = ((m + 1 + H) % R) // 2 == i // 2
+        same = (m - i) % C == 0
+        return (m % C == C - 1) | (same & beside if SAME == 1 else same if SAME else False)
 
     def send_turned(cond):
         for t in range(2):
@@ -192,9 +196,9 @@
             send(now & jnp.logical_not(crossing(r, m)) & (m >= 0) & target(r, m, 1), upper.at[:, slot(u)], an.at[to_u],
                  an_sem.at[to_u], (r, to))
 
-    def hand_down(u, rows):
+    def hand_down(u):
         m = c + C * u
-        live = rows & (r >= 1) & (r != H) & (m >= r) & target(r - 1, m, 1)
+        live = (r >= 1) & (r != H) & (m >= r) & target(r - 1, m, 1)
         to = (jnp.maximum(r - 1, 0), c)
         if u < U // 2:
             send(live & (m == r), upper.at[:, slot(u)], atb.at[1, u], at_sem.at[1, u], to)
@@ -230,15 +234,19 @@
         return pl.ds(PAD + h * half, half)
 
     def spread(s, h, who):
-        own_col = r % C == c
+        home = r % C
+        own_col = home == c
         k = jnp.where(own_col, r // C, (d[s] - r) // C)
-        has = (own_col | (c == o[s])) & who
+        has = (c == o[s]) & who if s > 0 and HOME else (own_col | (c == o[s])) & who
 
         def give(cond, to):
+            if s > 0 and HOME:
+                send(cond & has & (home != c), xz.at[s, U, part(h)], xz.at[s, r // C, part(h)],
+                     xz_sem.at[s, r // C, h], (to, home))
             send(cond & has, xz.at[s, U, part(h)], xz.at[s, k, part(h)], xz_sem.at[s, k, h], (to, c))
 
         give(r % 2 == 1, jnp.maximum(r - 1, 0))
-        for back in range(1, R // 2):
+        for back in range(R // 2 - 1, 0, -1) if s > 0 else range(1, R // 2):
             pair = r // 2 - back
             give(pair >= 0, jnp.maximum(2 * pair + 1 - r % 2, 0))
 
@@ -256,12 +264,9 @@
 
         if s == 0:
             give(True, goal)
-        else:
-            give(home != c, home)
         for h in range(PARTS):
             spread(s, h, at)
-        if s == 0:
-            give((home != goal) & (home != c), home)
+        give((home != c) & (home != goal) if s == 0 else home != c, home)
         for far_by in range(C - 1, 0, -1):
             for to in (c - far_by, c + far_by):
                 live = (to >= 0) & (to < C) & (to != home) & wants(to, s)
@@ -281,7 +286,8 @@
             def _(block=block, sem=sem):
                 arrive(block, sem)
 
-            spread(s, h, other)
+            if s == 0 or not HOME:
+                spread(s, h, other)
 
     def decoded(s, k):
         return decode(xz[s, k, PAD:], xz[s, k, 0:1, :].astype(F32))
@@ -396,17 +402,6 @@
             pl.when(straight)(lambda: apply(NN))
             pl.when(jnp.logical_not(straight))(lambda: apply(NT))
 
-    def on_targets(s, fns, but=None):
-        for u in range(U):
-            live = target(r, c + C * u, s)
-            if but is not None:
-                live = live & jnp.logical_not(but(u))
-
-            @pl.when(live)
-            def _(u=u):
-                for fn in fns:
-                    fn(u, s)
-
     hand_right = pltpu.make_async_remote_copy(
         src_ref=ops.at[1], dst_ref=ops.at[1], send_sem=send_sem.at[0], recv_sem=ops_sem.at[1],
         device_id=(jnp.maximum(r - 1, 0), c), device_id_type=MESH)
@@ -451,26 +446,44 @@
         give_row(1)
         send_upper(None, True)
 
-    def use_lower(rows):
-        with scope("hand"):
-            for u in range(U):
-                @pl.when(rows & needs(u) & jnp.logical_not(ahead & (top == u)))
-                def _(u=u):
-                    arrive(atb.at[0, u], at_sem.at[0, u])
-
-                hand_down(u, rows)
-        with scope("right0"):
-            on_targets(0, (right,), lambda u: picked(u) | jnp.logical_not(rows))
+    def at_hand(u, s):
+        j, k = z_index(u, s)
+        return (j == r) | ((r // 2 < j // 2) & (r % 2 != j % 2))
+
+    def use_right(s, u):
+        pl.when(target(r, c + C * u, s) & jnp.logical_not(picked(u) if s == 0 else False))(lambda: right(u, s))
+
+    def use_left(s, u, here):
+        live = target(r, c + C * u, s) & (at_hand(u, s) if here else jnp.logical_not(at_hand(u, s)))
+        if s == 0:
+            live = live & jnp.logical_not(picked(u))
+
+        @pl.when(live)
+        def _():
+            if s > 0:
+                arrive(an.at[u], an_sem.at[u])
+            left(u, s)
 
     with scope("direct0"):
         for u in range(U):
             collect(u, 0, True, jnp.logical_not(picked(u)))
-    use_lower(r >= 2)
-    with scope("collect0"):
-        for u in range(U):
+    with scope("leftA0"):
+        for u in range(U):
+            use_left(0, u, True)
+    with scope("hand"):
+        for u in range(U - 1, -1, -1):
+            @pl.when(needs(u) & jnp.logical_not(ahead & (top == u)))
+            def _(u=u):
+                arrive(atb.at[0, u], at_sem.at[0, u])
+
+            hand_down(u)
+    with scope("right0"):
+        for u in range(U):
+            use_right(0, u)
+    with scope("leftB0"):
+        for u in range(U - 1, -1, -1):
             collect(u, 0, False, jnp.logical_not(picked(u)))
-    with scope("left0"):
-        on_targets(0, (left,), picked)
+            use_left(0, u, False)
 
     with scope("take1"):
         take_row(1)
@@ -478,31 +491,21 @@
     with scope("direct1"):
         for u in range(U):
             collect(u, 1, True)
-    use_lower(r < 2)
-    with scope("w_an"):
-        for u in range(U):
-            @pl.when(target(r, c + C * u, 1))
-            def _(u=u):
-                arrive(an.at[u], an_sem.at[u])
+    with scope("leftA1"):
+        for u in range(U):
+            use_left(1, u, True)
     with scope("right1"):
-        on_targets(1, (right,))
-    for u in range(U):
-        with scope("collect1_%d" % u):
-            collect(u, 1, False)
-
-        @pl.when(target(r, c + C * u, 1))
-        def _(u=u):
-            with scope("left1_%d" % u):
-                left(u, 1)
-
-    def drain(some):
-        for cond, copy in some:
+        for u in range(U):
+            use_right(1, u)
+    with scope("drain"):
+        for cond, copy in sends:
             @pl.when(cond)
             def _(copy=copy):
                 copy.wait_send()
-
-    with scope("drain"):
-        drain(sends)
+    for u in range(U):
+        with scope("leftB1_%d" % u):
+            collect(u, 1, False)
+            use_left(1, u, False)
 
 
 def store(work, out, sem):

time: 33.7 us -> 31.7 us (0.941)
  Pallas kernels: 33.6 us -> 31.6 us
    pallas_call x1, Pallas kernels: 32.6 us -> 30.6 us  [on_device(): pl.pallas_call(functools.partial(kernel, R, C, U, BS, SR), out_shape=pltp...]
where the time goes in v6:
time: 31.7 us; the launch traced here: 31.6 us
  Pallas kernels  31.6 us (100%)
    pallas_call x1, Pallas kernels, on_device(): pl.pallas_call(functools.partial(kernel, R, C, U, BS, SR), out_shape=pltp...  30.6 us
    pallas_call x1, Pallas kernels, on_device(): pl.pallas_call(store, out_shape=jax.ShapeDtypeStruct((BS, flat // lanes,...  0.97 us

profile of v6, /device:TPU:0, one launch (start us, length us, event | category | flops | bytes accessed | tf_op | source)
XLA Modules:
  0.0 31.6 jit_solution(5848423976046384289)
XLA Ops:
  0.0 30.6 %shard_map.64.work = f32[256,1024]{1,0:T(8,128)S(1)} custom-call(f32[256,8,1,128]{3,2,1,0:T(1,128)} %bitcast.6, bf16[256,1024]{1,0:T(8,128)(2,1)} %bitcast.8, bf16[2,256,1024]{2,1,0:T(8,128)(2,1)} %bitcast.7, f32[4,32,256]{2,1,0:T(8,128)} %bitcast.9, f32[4,32,256]{2,1,0:T(8,128)} %bitcast.10, f32[4,1,256]{2,1,0:T(1,128)} %rates_in.1), custom_call_target="tpu_custom_call" | custom-call | tf_op jit(solution)/shard_map/pallas_call | solution.py:529
  30.6 1.0 %shard_map.65 = f32[256,8,1,128]{3,2,1,0:T(1,128)} custom-call(f32[256,1024]{1,0:T(8,128)S(1)} %shard_map.64.work), custom_call_target="tpu_custom_call" | custom-call | tf_op jit(solution)/shard_map/pallas_call | solution.py:566

commit v7 on v6

--- a/solution.py
+++ b/solution.py
@@ -12,6 +12,8 @@
 PAD = 16
 SAME = 2
 HOME = False
+RELAY = (False, False)
+FORWARD = True
 OP_MAX = 1.3
 MESH = pl.DeviceIdType.MESH
 F32 = jnp.float32
@@ -85,7 +87,7 @@
         copy = pltpu.make_async_remote_copy(
             src_ref=src, dst_ref=dst, send_sem=send_sem.at[0], recv_sem=sem,
             device_id=dev, device_id_type=MESH)
-        sends.append((cond, copy))
+        sends.append((cond, copy, (src.shape, str(src.dtype))))
 
         @pl.when(cond)
         def _():
@@ -127,7 +129,7 @@
             to = d[s] - (c + C * u)
             live = (to >= 0) & (to < R)
             if s > 0:
-                live = live & (to % 2 == 1)
+                live = live & (to % 4 == 3 if FORWARD else to % 2 == 1)
             send_or_local(live, enc.at[u], ops.at[1, r], ops_sem.at[1], (to, c))
 
     def send_lower(first):
@@ -200,9 +202,7 @@
         m = c + C * u
         live = (r >= 1) & (r != H) & (m >= r) & target(r - 1, m, 1)
         to = (jnp.maximum(r - 1, 0), c)
-        if u < U // 2:
-            send(live & (m == r), upper.at[:, slot(u)], atb.at[1, u], at_sem.at[1, u], to)
-        send(live & (m != r), atb.at[0, u], atb.at[1, u], at_sem.at[1, u], to)
+        send(live, atb.at[0, u], atb.at[1, u], at_sem.at[1, u], to)
 
     with scope("sends0"):
         send_left(0)
@@ -225,6 +225,10 @@
             arrive(atb.at[0, top], at_sem.at[0, top])
 
         send_turned(c != o[0])
+        for u in range(U // 2):
+            @pl.when(target(r, c + C * u, 0) & (c + C * u == r))
+            def _(u=u):
+                atb[0, u] = jnp.transpose(upper[:, slot(u)])
 
     half = BS // PARTS
 
@@ -247,6 +251,8 @@
 
         give(r % 2 == 1, jnp.maximum(r - 1, 0))
         for back in range(R // 2 - 1, 0, -1) if s > 0 else range(1, R // 2):
+            if back == 3 and RELAY[s]:
+                continue
             pair = r // 2 - back
             give(pair >= 0, jnp.maximum(2 * pair + 1 - r % 2, 0))
 
@@ -305,7 +311,7 @@
             with scope("w_op%d" % side):
                 arrive(ops.at[side], ops_sem.at[side])
             if s == 0 and side == 1:
-                pl.when(r % 2 == 1)(hand_right.start)
+                pl.when(hands)(hand_right.start)
             for k in range(0, R, group):
                 both = [decode(ops[side, k + i], OP_MAX) for i in range(group)]
                 for which in range(2):
@@ -352,44 +358,24 @@
 
             if direct:
                 send(landed, block, block, xz_sem.at[s, u, h], (r + 1 - 2 * (r % 2), c))
-
-    def right(u, s):
+                if RELAY[s]:
+                    on = landed & (r // 2 >= 1) & (j // 2 - r // 2 == 2)
+                    send(on, block, block, xz_sem.at[s, u, h], (jnp.maximum(r - 2, 0), c))
+
+    def update(u, s):
         m = c + C * u
-
-        def apply(a, dims):
-            out[:, slot(u)] -= mm(own[s, 0], a, dims) + mm(own[s, 1], a, dims)
-
-        def moved():
-            if s > 0:
+        j, k = z_index(u, s)
+
+        if s > 0:
+            @pl.when(m != r)
+            def _():
                 arrive(atb.at[s, u], at_sem.at[s, u])
 
-        if u >= U // 2:
-            moved()
-            apply(atb[s, u], NN)
-            return
-        plain = (m == r + 1) & (r != H - 1) if s > 0 else m < r
-
-        @pl.when(m == r)
-        def _():
-            apply(upper[:, slot(u)] if s == 0 else an[u], NT)
-
-        @pl.when((m != r) & plain)
-        def _():
-            moved()
-            apply(atb[s, u], NT)
-
-        @pl.when((m != r) & jnp.logical_not(plain))
-        def _():
-            moved()
-            apply(atb[s, u], NN)
-
-    def left(u, s):
-        j, k = z_index(u, s)
-        a = an[u] if s > 0 else upper[:, slot(u)]
-        zh, zl = halves(decoded(s, k))
-
         def apply(dims):
-            out[:, slot(u)] -= mm(a, zh, dims) + mm(a, zl, dims)
+            a = an[u] if s > 0 else upper[:, slot(u)]
+            zh, zl = halves(decoded(s, k))
+            row = mm(own[s, 0], atb[s, u], NN) + mm(own[s, 1], atb[s, u], NN)
+            out[:, slot(u)] -= row + (mm(a, zh, dims) + mm(a, zl, dims))
 
         low, high = C * u, C * u + C - 1
         if 2 * low >= d[s]:
@@ -397,7 +383,6 @@
         elif 2 * high < d[s]:
             apply(NT)
         else:
-            m = c + C * u
             straight = d[s] - m <= m
             pl.when(straight)(lambda: apply(NN))
             pl.when(jnp.logical_not(straight))(lambda: apply(NT))
@@ -405,7 +390,8 @@
     hand_right = pltpu.make_async_remote_copy(
         src_ref=ops.at[1], dst_ref=ops.at[1], send_sem=send_sem.at[0], recv_sem=ops_sem.at[1],
         device_id=(jnp.maximum(r - 1, 0), c), device_id_type=MESH)
-    sends.append(((c == o[0]) & (r % 2 == 1), hand_right))
+    hands = r % 4 != 0 if FORWARD else r % 2 == 1
+    sends.append(((c == o[0]) & hands, hand_right, ops.at[1].shape))
 
     @pl.when(c == o[0])
     def _():
@@ -434,8 +420,7 @@
 
             @pl.when(picked(u))
             def _(u=u):
-                right(u, 0)
-                left(u, 0)
+                update(u, 0)
 
     @pl.when(first)
     def _():
@@ -450,26 +435,15 @@
         j, k = z_index(u, s)
         return (j == r) | ((r // 2 < j // 2) & (r % 2 != j % 2))
 
-    def use_right(s, u):
-        pl.when(target(r, c + C * u, s) & jnp.logical_not(picked(u) if s == 0 else False))(lambda: right(u, s))
-
-    def use_left(s, u, here):
-        live = target(r, c + C * u, s) & (at_hand(u, s) if here else jnp.logical_not(at_hand(u, s)))
+    def use(s, u, here, also=True):
+        live = also & target(r, c + C * u, s) & (at_hand(u, s) if here else jnp.logical_not(at_hand(u, s)))
         if s == 0:
             live = live & jnp.logical_not(picked(u))
-
-        @pl.when(live)
-        def _():
-            if s > 0:
-                arrive(an.at[u], an_sem.at[u])
-            left(u, s)
+        pl.when(live)(lambda: update(u, s))
 
     with scope("direct0"):
-        for u in range(U):
+        for u in range(U - 1, -1, -1):
             collect(u, 0, True, jnp.logical_not(picked(u)))
-    with scope("leftA0"):
-        for u in range(U):
-            use_left(0, u, True)
     with scope("hand"):
         for u in range(U - 1, -1, -1):
             @pl.when(needs(u) & jnp.logical_not(ahead & (top == u)))
@@ -477,35 +451,56 @@
                 arrive(atb.at[0, u], at_sem.at[0, u])
 
             hand_down(u)
-    with scope("right0"):
+    with scope("A0"):
         for u in range(U):
-            use_right(0, u)
-    with scope("leftB0"):
+            use(0, u, True)
+    with scope("B0"):
         for u in range(U - 1, -1, -1):
             collect(u, 0, False, jnp.logical_not(picked(u)))
-            use_left(0, u, False)
+            use(0, u, False)
 
     with scope("take1"):
         take_row(1)
         pl.when(wants(c, 1))(lambda: split_own(1))
     with scope("direct1"):
+        for u in range(U - 1, -1, -1):
+            collect(u, 1, True)
+    with scope("w_an"):
         for u in range(U):
-            collect(u, 1, True)
-    with scope("leftA1"):
+            m = c + C * u
+
+            @pl.when(target(r, m, 1))
+            def _(u=u):
+                arrive(an.at[u], an_sem.at[u])
+
+            if u < U // 2:
+                @pl.when(target(r, m, 1) & (m == r))
+                def _(u=u):
+                    atb[1, u] = jnp.transpose(an[u])
+    with scope("A1"):
         for u in range(U):
-            use_left(1, u, True)
-    with scope("right1"):
-        for u in range(U):
-            use_right(1, u)
+            use(1, u, True)
     with scope("drain"):
-        for cond, copy in sends:
-            @pl.when(cond)
-            def _(copy=copy):
+        sizes = {}
+        for cond, copy, size in sends:
+            sizes.setdefault(size, []).append((cond, copy))
+        for group in sizes.values():
+            count = sum(jnp.where(cond, 1, 0) for cond, _ in group)
+
+            @pl.loop(0, count)
+            def _(_, copy=group[0][1]):
                 copy.wait_send()
-    for u in range(U):
-        with scope("leftB1_%d" % u):
+    def twice(u):
+        j, k = z_index(u, 1)
+        return (u >= U // 2) & (j % C == c)
+
+    for u in range(U - 1, -1, -1):
+        with scope("B1_%d" % u):
             collect(u, 1, False)
-            use_left(1, u, False)
+            use(1, u, False, jnp.logical_not(twice(u)))
+    for u in range(U // 2, U):
+        with scope("C1_%d" % u):
+            use(1, u, False, twice(u))
 
 
 def store(work, out, sem):

time: 31.7 us -> 31 us (0.978)
  Pallas kernels: 31.6 us -> 30.9 us
    pallas_call x1, Pallas kernels: 30.6 us -> 29.9 us  [on_device(): pl.pallas_call(functools.partial(kernel, R, C, U, BS, SR), out_shape=pltp...]
where the time goes in v7:
time: 31 us; the launch traced here: 30.9 us
  Pallas kernels  30.9 us (100%)
    pallas_call x1, Pallas kernels, on_device(): pl.pallas_call(functools.partial(kernel, R, C, U, BS, SR), out_shape=pltp...  29.9 us
    pallas_call x1, Pallas kernels, on_device(): pl.pallas_call(store, out_shape=jax.ShapeDtypeStruct((BS, flat // lanes,...  0.97 us

profile of v7, /device:TPU:0, one launch (start us, length us, event | category | flops | bytes accessed | tf_op | source)
XLA Modules:
  0.0 30.9 jit_solution(9105270074737402691)
XLA Ops:
  0.0 29.9 %shard_map.64.work = f32[256,1024]{1,0:T(8,128)S(1)} custom-call(f32[256,8,1,128]{3,2,1,0:T(1,128)} %bitcast.6, bf16[256,1024]{1,0:T(8,128)(2,1)} %bitcast.8, bf16[2,256,1024]{2,1,0:T(8,128)(2,1)} %bitcast.7, f32[4,32,256]{2,1,0:T(8,128)} %bitcast.9, f32[4,32,256]{2,1,0:T(8,128)} %bitcast.10, f32[4,1,256]{2,1,0:T(1,128)} %rates_in.1), custom_call_target="tpu_custom_call" | custom-call | tf_op jit(solution)/shard_map/pallas_call | solution.py:524
  29.9 1.0 %shard_map.65 = f32[256,8,1,128]{3,2,1,0:T(1,128)} custom-call(f32[256,1024]{1,0:T(8,128)S(1)} %shard_map.64.work), custom_call_target="tpu_custom_call" | custom-call | tf_op jit(solution)/shard_map/pallas_call | solution.py:561

commit v8 on v7

--- a/solution.py
+++ b/solution.py
@@ -8,10 +8,11 @@
 from jax.sharding import PartitionSpec as P
 
 STEPS = 2
-PARTS = 2
+PARTS = 4
 PAD = 16
 SAME = 2
 HOME = False
+MIX = True
 RELAY = (False, False)
 FORWARD = True
 OP_MAX = 1.3
@@ -241,16 +242,17 @@
         home = r % C
         own_col = home == c
         k = jnp.where(own_col, r // C, (d[s] - r) // C)
-        has = (c == o[s]) & who if s > 0 and HOME else (own_col | (c == o[s])) & who
+        straight = home == 0 if s > 0 and HOME else False
+        has = (own_col & jnp.logical_not(straight) | (c == o[s])) & who
 
         def give(cond, to):
             if s > 0 and HOME:
-                send(cond & has & (home != c), xz.at[s, U, part(h)], xz.at[s, r // C, part(h)],
-                     xz_sem.at[s, r // C, h], (to, home))
+                send(cond & who & straight & (c == o[s]) & (home != c), xz.at[s, U, part(h)],
+                     xz.at[s, r // C, part(h)], xz_sem.at[s, r // C, h], (to, home))
             send(cond & has, xz.at[s, U, part(h)], xz.at[s, k, part(h)], xz_sem.at[s, k, h], (to, c))
 
         give(r % 2 == 1, jnp.maximum(r - 1, 0))
-        for back in range(R // 2 - 1, 0, -1) if s > 0 else range(1, R // 2):
+        for back in range(R // 2 - 1, 0, -1) if s > 0 and HOME else range(1, R // 2):
             if back == 3 and RELAY[s]:
                 continue
             pair = r // 2 - back
@@ -268,11 +270,11 @@
                 block = xz.at[s, U, part(h)]
                 send(at & cond, block, block, xz_sem.at[s, U, h], (r, jnp.clip(to, 0, C - 1)))
 
-        if s == 0:
-            give(True, goal)
+        give(True if s == 0 else home != c, goal if s == 0 else home)
         for h in range(PARTS):
             spread(s, h, at)
-        give((home != c) & (home != goal) if s == 0 else home != c, home)
+        if s == 0:
+            give((home != c) & (home != goal), home)
         for far_by in range(C - 1, 0, -1):
             for to in (c - far_by, c + far_by):
                 live = (to >= 0) & (to < C) & (to != home) & wants(to, s)
@@ -292,8 +294,7 @@
             def _(block=block, sem=sem):
                 arrive(block, sem)
 
-            if s == 0 or not HOME:
-                spread(s, h, other)
+            spread(s, h, other)
 
     def decoded(s, k):
         return decode(xz[s, k, PAD:], xz[s, k, 0:1, :].astype(F32))
@@ -459,10 +460,14 @@
             collect(u, 0, False, jnp.logical_not(picked(u)))
             use(0, u, False)
 
+    def twice(u):
+        j, k = z_index(u, 1)
+        return (u >= U // 2) & (j % C == c)
+
     with scope("take1"):
         take_row(1)
         pl.when(wants(c, 1))(lambda: split_own(1))
-    with scope("direct1"):
+    if not MIX:
         for u in range(U - 1, -1, -1):
             collect(u, 1, True)
     with scope("w_an"):
@@ -477,9 +482,17 @@
                 @pl.when(target(r, m, 1) & (m == r))
                 def _(u=u):
                     atb[1, u] = jnp.transpose(an[u])
+    if MIX:
+        for u in range(U - 1, -1, -1):
+            with scope("direct1_%d" % u):
+                collect(u, 1, True)
+            with scope("A1_%d" % u):
+                use(1, u, True, jnp.logical_not(twice(u)))
     with scope("A1"):
         for u in range(U):
-            use(1, u, True)
+            if MIX and u < U // 2:
+                continue
+            use(1, u, True, twice(u) if MIX else True)
     with scope("drain"):
         sizes = {}
         for cond, copy, size in sends:
@@ -490,10 +503,6 @@
             @pl.loop(0, count)
             def _(_, copy=group[0][1]):
                 copy.wait_send()
-    def twice(u):
-        j, k = z_index(u, 1)
-        return (u >= U // 2) & (j % C == c)
-
     for u in range(U - 1, -1, -1):
         with scope("B1_%d" % u):
             collect(u, 1, False)

time: 31 us -> 30.7 us (level)
    pallas_call x1, Pallas kernels: 29.9 us -> 29.6 us  [on_device(): pl.pallas_call(functools.partial(kernel, R, C, U, BS, SR), out_shape=pltp...]
where the time goes in v8:
time: 30.7 us; the launch traced here: 30.6 us
  Pallas kernels  30.6 us (100%)
    pallas_call x1, Pallas kernels, on_device(): pl.pallas_call(functools.partial(kernel, R, C, U, BS, SR), out_shape=pltp...  29.6 us
    pallas_call x1, Pallas kernels, on_device(): pl.pallas_call(store, out_shape=jax.ShapeDtypeStruct((BS, flat // lanes,...  0.97 us

profile of v8, /device:TPU:0, one launch (start us, length us, event | category | flops | bytes accessed | tf_op | source)
XLA Modules:
  0.0 30.6 jit_solution(2175214506910866616)
XLA Ops:
  0.0 29.6 %shard_map.64.work = f32[256,1024]{1,0:T(8,128)S(1)} custom-call(f32[256,8,1,128]{3,2,1,0:T(1,128)} %bitcast.6, bf16[256,1024]{1,0:T(8,128)(2,1)} %bitcast.8, bf16[2,256,1024]{2,1,0:T(8,128)(2,1)} %bitcast.7, f32[4,32,256]{2,1,0:T(8,128)} %bitcast.9, f32[4,32,256]{2,1,0:T(8,128)} %bitcast.10, f32[4,1,256]{2,1,0:T(1,128)} %rates_in.1), custom_call_target="tpu_custom_call" | custom-call | tf_op jit(solution)/shard_map/pallas_call | solution.py:533
  29.6 1.0 %shard_map.65 = f32[256,8,1,128]{3,2,1,0:T(1,128)} custom-call(f32[256,1024]{1,0:T(8,128)S(1)} %shard_map.64.work), custom_call_target="tpu_custom_call" | custom-call | tf_op jit(solution)/shard_map/pallas_call | solution.py:570

commit v9 on v8

--- a/solution.py
+++ b/solution.py
@@ -121,7 +121,7 @@
         pl.semaphore_wait(barrier, R * C - 1)
 
     def send_left(s):
-        for u in range(U // 2):
+        for u in range(U // 2 - 1, -1, -1):
             m = c + C * u
             send_or_local(m < R, enc.at[u], ops.at[0, r], ops_sem.at[0], (m, owner(m, s)))
 

time: 30.7 us -> 30.6 us (level)
  the two profiles are of different devices: /device:TPU:0 before, /device:TPU:9 now
where the time goes in v9:
time: 30.6 us; the launch traced here: 30.5 us
  Pallas kernels  30.5 us (100%)
    pallas_call x1, Pallas kernels, on_device(): pl.pallas_call(functools.partial(kernel, R, C, U, BS, SR), out_shape=pltp...  29.5 us
    pallas_call x1, Pallas kernels, on_device(): pl.pallas_call(store, out_shape=jax.ShapeDtypeStruct((BS, flat // lanes,...  0.97 us

profile of v9, /device:TPU:9, one launch (start us, length us, event | category | flops | bytes accessed | tf_op | source)
XLA Modules:
  0.0 30.5 jit_solution(2509009839961680070)
XLA Ops:
  0.0 29.5 %shard_map.64.work = f32[256,1024]{1,0:T(8,128)S(1)} custom-call(f32[256,8,1,128]{3,2,1,0:T(1,128)} %bitcast.6, bf16[256,1024]{1,0:T(8,128)(2,1)} %bitcast.8, bf16[2,256,1024]{2,1,0:T(8,128)(2,1)} %bitcast.7, f32[4,32,256]{2,1,0:T(8,128)} %bitcast.9, f32[4,32,256]{2,1,0:T(8,128)} %bitcast.10, f32[4,1,256]{2,1,0:T(1,128)} %rates_in.1), custom_call_target="tpu_custom_call" | custom-call | tf_op jit(solution)/shard_map/pallas_call | solution.py:533
  29.5 1.0 %shard_map.65 = f32[256,8,1,128]{3,2,1,0:T(1,128)} custom-call(f32[256,1024]{1,0:T(8,128)S(1)} %shard_map.64.work), custom_call_target="tpu_custom_call" | custom-call | tf_op jit(solution)/shard_map/pallas_call | solution.py:570
